TPU v7x, 8 devices: a whole 2x2x1 slice. The times are simulated.
8 devices in a mesh: dp: 1 (over z), tp: 2 (over y), cp: 4 (over x, core).
Axes of the slice: x: 2, y: 2, z: 1, core: 2. Of those that a mesh axis runs over, the one named last changes fastest.
Arguments:
- hidden_in: bfloat16 [256, 2048], P(('dp', 'cp', 'tp'))
- positions: int32 [256], P(('dp', 'cp', 'tp'))
- cache_len: int32 [1], P('dp')
- cache_k: bfloat16 [32768, 256], P(('dp', 'cp', 'tp'))
- cache_v: bfloat16 [32768, 256], P(('dp', 'cp', 'tp'))
- norm1_gain: bfloat16 [2048], replicated
- w_query: bfloat16 [2048, 2048], P(None, 'tp')
- w_key: bfloat16 [2048, 256], P(None, 'tp')
- w_value: bfloat16 [2048, 256], P(None, 'tp')
- w_out: bfloat16 [2048, 2048], P('tp')
- norm2_gain: bfloat16 [2048], replicated
- w_gate: bfloat16 [2048, 11008], P(None, 'tp')
- w_up: bfloat16 [2048, 11008], P(None, 'tp')
- w_down: bfloat16 [11008, 2048], P('tp')
Outputs:
- output: bfloat16 [256, 2048], P(('dp', 'cp', 'tp'))
All inputs are finite; a program needn't handle non-finite values.
Results may differ from a plain program's by a relative error of at most 0.0110318.
Values are sent between devices in bfloat16 or wider.
A program may use at most 1 GiB of HBM per device.

v0:
```python
import math
import jax
import jax.numpy as jnp
from jax import lax
from jax.sharding import PartitionSpec as P

HEAD_DIM = 128
ROPE_BASE = 500000.0
NORM_EPS = 1e-5


def rms_norm(hidden, norm_gain):
    values = hidden.astype(jnp.float32)
    inv_rms = lax.rsqrt(jnp.mean(values * values, axis=-1, keepdims=True) + NORM_EPS)
    return (values * inv_rms * norm_gain.astype(jnp.float32)).astype(jnp.bfloat16)


def rotary(projected, positions):
    half_dim = HEAD_DIM // 2
    inv_freq = 1.0 / (ROPE_BASE ** (jnp.arange(half_dim, dtype=jnp.float32) * (2.0 / HEAD_DIM)))
    angles = positions.astype(jnp.float32)[:, None] * inv_freq[None, :]
    expand = (angles.shape[0],) + (1,) * (projected.ndim - 2) + (half_dim,)
    cos_table = jnp.cos(angles).reshape(expand)
    sin_table = jnp.sin(angles).reshape(expand)
    first_half = projected[..., :half_dim]
    second_half = projected[..., half_dim:]
    rotated = jnp.concatenate([first_half * cos_table - second_half * sin_table, second_half * cos_table + first_half * sin_table], axis=-1)
    return rotated.astype(jnp.bfloat16)


def attend_rows(block_queries, block_pos, cache_keys, cache_values, cache_valid, new_keys, new_values, all_pos):
    score_scale = 1.0 / math.sqrt(HEAD_DIM)
    cache_scores = jnp.einsum('rkgd,skd->krgs', block_queries, cache_keys, preferred_element_type=jnp.float32) * score_scale
    new_scores = jnp.einsum('rkgd,skd->krgs', block_queries, new_keys, preferred_element_type=jnp.float32) * score_scale
    cache_scores = jnp.where(cache_valid, cache_scores, -jnp.inf)
    causal = all_pos[None, None, None, :] <= block_pos[None, :, None, None]
    new_scores = jnp.where(causal, new_scores, -jnp.inf)
    row_max = jnp.maximum(jnp.max(cache_scores, axis=-1, keepdims=True), jnp.max(new_scores, axis=-1, keepdims=True))
    cache_probs = jnp.exp(cache_scores - row_max)
    new_probs = jnp.exp(new_scores - row_max)
    normalizer = jnp.sum(cache_probs, axis=-1, keepdims=True) + jnp.sum(new_probs, axis=-1, keepdims=True)
    weighted = jnp.einsum('krgs,skd->krgd', cache_probs.astype(jnp.bfloat16), cache_values, preferred_element_type=jnp.float32)
    weighted = weighted + jnp.einsum('krgs,skd->krgd', new_probs.astype(jnp.bfloat16), new_values, preferred_element_type=jnp.float32)
    return jnp.transpose((weighted / normalizer).astype(jnp.bfloat16), (1, 0, 2, 3))


def solution(mesh):
    tp_size = mesh.shape['tp']
    token_spec = P(('dp', 'cp', 'tp'), None)
    column_spec = P(None, 'tp')
    row_spec = P('tp', None)

    def device_layer(hidden_loc, pos_loc, cache_len, cache_k, cache_v, norm1_gain, w_query, w_key, w_value, w_out, norm2_gain, w_gate, w_up, w_down):
        shard_rows = hidden_loc.shape[0]
        kv_local = w_key.shape[1] // HEAD_DIM
        groups = w_query.shape[1] // w_key.shape[1]
        normed = rms_norm(hidden_loc, norm1_gain)
        group_in = lax.all_gather(normed, 'tp', axis=0, tiled=True)
        group_pos = lax.all_gather(pos_loc, 'tp', axis=0, tiled=True)
        group_rows = group_in.shape[0]
        queries = rotary(jnp.dot(group_in, w_query, preferred_element_type=jnp.float32).reshape(group_rows, kv_local, groups, HEAD_DIM), group_pos)
        keys_loc = rotary(jnp.dot(group_in, w_key, preferred_element_type=jnp.float32).reshape(group_rows, kv_local, HEAD_DIM), group_pos)
        values_loc = jnp.dot(group_in, w_value, preferred_element_type=jnp.float32).astype(jnp.bfloat16).reshape(group_rows, kv_local, HEAD_DIM)
        new_keys = lax.all_gather(keys_loc, 'cp', axis=0, tiled=True)
        new_values = lax.all_gather(values_loc, 'cp', axis=0, tiled=True)
        all_pos = lax.all_gather(group_pos, 'cp', axis=0, tiled=True)
        cache_keys = lax.all_gather(lax.all_to_all(cache_k, 'tp', 1, 0, tiled=True), 'cp', axis=0, tiled=True).reshape(-1, kv_local, HEAD_DIM)
        cache_values = lax.all_gather(lax.all_to_all(cache_v, 'tp', 1, 0, tiled=True), 'cp', axis=0, tiled=True).reshape(-1, kv_local, HEAD_DIM)
        cache_valid = jnp.arange(cache_keys.shape[0]) < cache_len[0]
        block_queries = queries.reshape(tp_size, shard_rows, kv_local, groups, HEAD_DIM)
        block_pos = group_pos.reshape(tp_size, shard_rows)

        def attend_block(block_item):
            return attend_rows(block_item[0], block_item[1], cache_keys, cache_values, cache_valid, new_keys, new_values, all_pos)

        attended = lax.map(attend_block, (block_queries, block_pos)).reshape(group_rows, kv_local * groups * HEAD_DIM)
        attn_part = jnp.dot(attended, w_out, preferred_element_type=jnp.float32)
        residual_mid = (hidden_loc.astype(jnp.float32) + lax.psum_scatter(attn_part, 'tp', scatter_dimension=0, tiled=True)).astype(jnp.bfloat16)
        group_mid = lax.all_gather(rms_norm(residual_mid, norm2_gain), 'tp', axis=0, tiled=True)
        gate_proj = jnp.dot(group_mid, w_gate, preferred_element_type=jnp.float32)
        up_proj = jnp.dot(group_mid, w_up, preferred_element_type=jnp.float32)
        hidden_mlp = (jax.nn.silu(gate_proj) * up_proj).astype(jnp.bfloat16)
        mlp_part = jnp.dot(hidden_mlp, w_down, preferred_element_type=jnp.float32)
        return (residual_mid.astype(jnp.float32) + lax.psum_scatter(mlp_part, 'tp', scatter_dimension=0, tiled=True)).astype(jnp.bfloat16)

    return jax.shard_map(device_layer, mesh=mesh, in_specs=(token_spec, P(('dp', 'cp', 'tp')), P('dp'), token_spec, token_spec, P(), column_spec, column_spec, column_spec, row_spec, P(), column_spec, column_spec, row_spec), out_specs=token_spec, check_vma=False)
```

profile of v0, /device:TPU:0, one launch (start us, length us, event | category | flops | bytes accessed | tf_op | source)
XLA Modules:
  0.0 320.2 jit_solution(7169295796081060761)
XLA Ops:
  6.5 1.6 copy-done
  8.1 0.1 copy_bitcast_fusion
  8.3 0.0 copy-start.12
  8.3 30.2 %all_to_all.38 = bf16[4096,2,128]{2,0,1:T(8,128)(2,1)} all-to-all(bf16[4096,2,128]{2,0,1:T(8,128)(2,1)S(1)} %copy_bitcast_fusion), channel_id=1, replica_groups=mesh['dp'=1,'tp'=2,'cp'=4] {'tp'}, dimensions={1} | all-to-all | bytes 4194304 | tf_op jit(solution)/shard_map/all_to_all | solution.py:68
  38.5 0.0 all-gather.6.cloned.1.call-update
  38.6 0.0 copy-start.11
  38.6 0.0 all-gather.4.cloned.1.call-start
  38.6 2.0 copy_bitcast_fusion.1
  40.7 28.0 %all_to_all.39 = bf16[4096,2,128]{2,0,1:T(8,128)(2,1)} all-to-all(bf16[4096,2,128]{2,0,1:T(8,128)(2,1)S(1)} %copy_bitcast_fusion.1), channel_id=1, replica_groups=mesh['dp'=1,'tp'=2,'cp'=4] {'tp'}, dimensions={1} | all-to-all | bytes 4194304 | tf_op jit(solution)/shard_map/all_to_all | solution.py:67
  68.6 0.0 all-gather.4.cloned.1.call-update
  68.7 0.0 reduce-scatter.3.cloned.1.call-start
  68.7 0.6 dynamic-slice
  69.9 0.2 dynamic-update-slice
  70.1 4.3 %all-reduce = s32[64]{0:T(128)S(1)} all-reduce(s32[64]{0:T(128)S(1)} %dynamic-update-slice), channel_id=1, replica_groups=mesh['dp'=1,'tp'=2,'cp'=4] {'tp'}, use_global_device_ids=true, to_apply=%add | all-reduce | flops 64 | bytes 512
  74.4 0.1 reshape.359
  74.5 0.1 fusion.35
  74.6 0.1 fusion.37
  74.8 5.6 %all_gather.24 = bf16[64,2048]{1,0:T(8,128)(2,1)S(1)} all-gather(bf16[32,2048]{1,0:T(8,128)(2,1)S(1)} %fusion.37), channel_id=1, replica_groups=mesh['dp'=1,'tp'=2,'cp'=4] {'tp'}, dimensions={0}, use_global_device_ids=true | all-gather | bytes 393216 | tf_op jit(solution)/shard_map/all_gather | solution.py:58
  80.4 3.0 convolution_bitcast_fusion
  83.5 0.6 dynamic-slice.1
  84.7 0.2 dynamic-update-slice.1
  84.9 4.9 %all-reduce.1 = s32[256]{0:T(256)S(1)} all-reduce(s32[256]{0:T(256)S(1)} %dynamic-update-slice.1), channel_id=1, replica_groups=mesh['dp'=1,'tp'=2,'cp'=4] {'cp'}, use_global_device_ids=true, to_apply=%add.1 | all-reduce | flops 256 | bytes 2048
  89.8 0.2 convolution_bitcast_fusion.1
  90.0 0.2 fusion.51
  90.2 0.1 pad_maximum_fusion.1
  90.3 7.6 %all_gather.28 = bf16[256,1,128]{2,0,1:T(8,128)(2,1)S(1)} all-gather(bf16[64,1,128]{2,0,1:T(8,128)(2,1)S(1)} %pad_maximum_fusion.1), channel_id=1, replica_groups=mesh['dp'=1,'tp'=2,'cp'=4] {'cp'}, dimensions={0}, use_global_device_ids=true | all-gather | bytes 81920 | tf_op jit(solution)/shard_map/all_gather | solution.py:64
  97.9 0.2 convolution_convert_fusion
  98.1 8.1 %all-gather = bf16[256,128]{1,0:T(8,128)(2,1)S(1)} all-gather(bf16[64,128]{1,0:T(8,128)(2,1)S(1)} %convolution_convert_fusion), channel_id=2, replica_groups=mesh['dp'=1,'tp'=2,'cp'=4] {'cp'}, dimensions={0}, use_global_device_ids=true | all-gather | bytes 81920 | tf_op jit(solution)/shard_map/all_gather | solution.py:65
  106.2 0.2 multiply_cosine_fusion.1
  106.4 0.2 subtract_convert_fusion
  106.6 0.1 pad_maximum_fusion
  106.7 0.0 all-gather.6.cloned.1.call-done
  106.7 45.6 %all-gather.4.cloned.1.call-done = bf16[32768,128]{1,0:T(8,128)(2,1)} async-done(((bf16[8192,128]{1,0:T(8,128)(2,1)}), bf16[32768,128]{1,0:T(8,128)(2,1)}) %all-gather.4.cloned.1.call-update) | async-done | bytes 8388624 | tf_op jit(solution)/shard_map/all_gather | solution.py:67
  152.3 95.2 %while.11 = (s32[]{:T(128)}, bf16[2,32,1,8,128]{4,3,1,2,0:T(8,128)(2,1)S(1)}, bf16[2,32,1,8,128]{4,3,1,2,0:T(8,128)(2,1)S(1)}, bf16[32768,1,128]{2,0,1:T(8,128)(...) while((s32[]{:T(128)}, ...), condition=%wide.region_6.7_spmd.clone, body=%wide.region_1.6_spmd.clone.sunk | while | flops 4387840000 | bytes 118946304 | solution.py:76
  152.3 0.1 broadcast_compare_fusion.2
  152.4 0.3 fusion.90
  152.7 0.7 iota_compare_fusion.2
  153.3 16.5 %fusion.88 = (f32[32,8]{1,0:T(8,128)S(1)}, f32[32,8,32768]{2,1,0:T(8,128)}) fusion(bf16[32768,1,128]{2,0,1:T(8,128)(2,1)} %get-tuple-element.207, bf16[2,32,1,8,128]{4,3,1,2,0:T(8,128)(2,1)S(1)} %get-tuple-element.206, s32[]{:T(128)} %get-tuple-element.193, pred[32768]{0:T(1024)(128)(4,1)S(1)} %iota_compare_fusion.2), kind=kOutput, calls=%fused_computation.83.clone.1 | convolution fusion | flops 2172649216 | bytes 42042372 | tf_op jit(solution)/shard_map/while/body/eval_jaxpr/rkgd,skd->krgs/dot_general | solution.py:33
  169.8 0.2 fusion.93
  170.0 14.0 %fusion.92 = f32[32,8]{1,0:T(8,128)S(1)} fusion(f32[32,8,32768]{2,1,0:T(8,128)} %get-tuple-element.178, f32[32,8]{1,0:T(8,128)S(1)} %max.10), kind=kLoop, calls=%fused_computation.4.clone.1 | loop fusion | flops 16776960 | bytes 33556480 | tf_op jit(solution)/shard_map/while/body/eval_jaxpr/reduce_sum | solution.py:41
  184.1 15.6 %fusion.91 = f32[32,8,128]{2,1,0:T(8,128)S(1)} fusion(f32[32,8,32768]{2,1,0:T(8,128)} %get-tuple-element.178, f32[32,8]{1,0:T(8,128)S(1)} %max.10, bf16[32768,1,128]{2,0,1:T(8,128)(2,1)} %get-tuple-element.211), kind=kOutput, calls=%fused_computation.6.clone.1 | convolution fusion | flops 2164260864 | bytes 42075136 | tf_op jit(solution)/shard_map/while/body/eval_jaxpr/krgs,skd->krgd/dot_general | solution.py:42
  199.6 0.3 fusion.94
  199.9 0.1 broadcast_compare_fusion.2
  200.0 0.3 fusion.90
  200.3 0.7 iota_compare_fusion.2
  201.0 16.5 %fusion.88 = (f32[32,8]{1,0:T(8,128)S(1)}, f32[32,8,32768]{2,1,0:T(8,128)}) fusion(bf16[32768,1,128]{2,0,1:T(8,128)(2,1)} %get-tuple-element.207, bf16[2,32,1,8,128]{4,3,1,2,0:T(8,128)(2,1)S(1)} %get-tuple-element.206, s32[]{:T(128)} %get-tuple-element.193, pred[32768]{0:T(1024)(128)(4,1)S(1)} %iota_compare_fusion.2), kind=kOutput, calls=%fused_computation.83.clone.1 | convolution fusion | flops 2172649216 | bytes 42042372 | tf_op jit(solution)/shard_map/while/body/eval_jaxpr/rkgd,skd->krgs/dot_general | solution.py:33
  217.5 0.2 fusion.93
  217.7 14.0 %fusion.92 = f32[32,8]{1,0:T(8,128)S(1)} fusion(f32[32,8,32768]{2,1,0:T(8,128)} %get-tuple-element.178, f32[32,8]{1,0:T(8,128)S(1)} %max.10), kind=kLoop, calls=%fused_computation.4.clone.1 | loop fusion | flops 16776960 | bytes 33556480 | tf_op jit(solution)/shard_map/while/body/eval_jaxpr/reduce_sum | solution.py:41
  231.7 15.6 %fusion.91 = f32[32,8,128]{2,1,0:T(8,128)S(1)} fusion(f32[32,8,32768]{2,1,0:T(8,128)} %get-tuple-element.178, f32[32,8]{1,0:T(8,128)S(1)} %max.10, bf16[32768,1,128]{2,0,1:T(8,128)(2,1)} %get-tuple-element.211), kind=kOutput, calls=%fused_computation.6.clone.1 | convolution fusion | flops 2164260864 | bytes 42075136 | tf_op jit(solution)/shard_map/while/body/eval_jaxpr/krgs,skd->krgd/dot_general | solution.py:42
  247.3 0.3 fusion.94
  247.5 3.8 %fusion.43 = f32[64,2048]{1,0:T(8,128)} fusion(bf16[1024,2048]{1,0:T(8,128)(2,1)} %param.25, bf16[8,8,8,128]{3,2,1,0:T(8,128)(2,1)S(1)} %bitcast.107), kind=kOutput, calls=%fused_computation.62 | convolution fusion | flops 268435456 | bytes 4849664 | tf_op jit(solution)/shard_map/dot_general | solution.py:77
  251.4 0.0 reduce-scatter.3.cloned.1.call-update
  251.4 0.0 reduce-scatter.5.cloned.1.call-start
  251.5 11.7 %reduce-scatter.3.cloned.1.call-done = f32[32,2048]{1,0:T(8,128)} async-done(((f32[64,2048]{1,0:T(8,128)}), f32[32,2048]{1,0:T(8,128)}) %reduce-scatter.3.cloned.1.call-update) | async-done | bytes 262160 | tf_op jit(solution)/shard_map/reduce_scatter | solution.py:78
  263.1 1.1 fusion.39
  264.2 0.6 copy-done.5
  264.9 0.1 fusion.41
  265.0 5.8 %all_gather.31 = bf16[64,2048]{1,0:T(8,128)(2,1)S(1)} all-gather(bf16[32,2048]{1,0:T(8,128)(2,1)S(1)} %fusion.41), channel_id=1, replica_groups=mesh['dp'=1,'tp'=2,'cp'=4] {'tp'}, dimensions={0}, use_global_device_ids=true | all-gather | bytes 393216 | tf_op jit(solution)/shard_map/all_gather | solution.py:79
  270.8 0.7 copy-done.2
  271.5 9.5 %fusion.58 = f32[64,5504]{1,0:T(8,128)S(1)} fusion(bf16[64,2048]{1,0:T(8,128)(2,1)S(1)} %all_gather.31, bf16[2048,5504]{1,0:T(8,128)(2,1)} %param.27), kind=kOutput, calls=%fused_computation.85 | convolution fusion | flops 1442840576 | bytes 24215552 | tf_op jit(solution)/shard_map/dot_general | solution.py:80
  281.0 19.0 %fusion.29 = f32[64,2048]{1,0:T(8,128)} fusion(bf16[5504,2048]{1,0:T(8,128)(2,1)} %param.29, bf16[64,2048]{1,0:T(8,128)(2,1)} %copy-done.2, bf16[2048,5504]{1,0:T(8,128)(2,1)} %param.28, f32[64,5504]{1,0:T(8,128)S(1)} %fusion.58), kind=kOutput, calls=%fused_computation.37 | convolution fusion | flops 2887794688 | bytes 47284224 | tf_op jit(solution)/shard_map/dot_general | solution.py:83
  300.1 0.0 reduce-scatter.5.cloned.1.call-update
  300.1 11.9 %reduce-scatter.5.cloned.1.call-done = f32[32,2048]{1,0:T(8,128)} async-done(((f32[64,2048]{1,0:T(8,128)}), f32[32,2048]{1,0:T(8,128)}) %reduce-scatter.5.cloned.1.call-update) | async-done | bytes 262160 | tf_op jit(solution)/shard_map/reduce_scatter | solution.py:84
  312.0 1.7 fusion.42
  (38 shorter events, 0.2 us)
Async XLA Ops:
  6.5 1.6 copy-start
  6.5 100.2 %all-gather.6.cloned.1.call-start = ((), (), s32[]{:S(2)}) async-start(), calls=%async_computation.5 | async-start | bytes 10485760 | tf_op jit(solution)/shard_map/all_gather | solution.py:68
  8.3 60.5 %copy-start.12 = (u32[8]{0:T(128)S(1)}, u32[8]{0:T(128)}, u32[]{:S(2)}) copy-start(u32[8]{0:T(128)} %constant.40) | copy-start | bytes 100
  8.3 61.6 %copy-start.10 = (s32[32]{0:T(128)S(1)}, s32[32]{0:T(128)}, u32[]{:S(2)}) copy-start(s32[32]{0:T(128)} %param.17) | copy-start | bytes 388
  8.3 66.2 %copy-start.8 = (bf16[2048]{0:T(1024)(128)(2,1)S(1)}, bf16[2048]{0:T(1024)(128)(2,1)}, u32[]{:S(2)}) copy-start(bf16[2048]{0:T(1024)(128)(2,1)} %param.21) | copy-start | bytes 12292
  8.3 66.2 %copy-start.3 = (bf16[32,2048]{1,0:T(8,128)(2,1)S(1)}, bf16[32,2048]{1,0:T(8,128)(2,1)}, u32[]{:S(2)}) copy-start(bf16[32,2048]{1,0:T(8,128)(2,1)} %param.16) | copy-start | bytes 393220
  38.6 44.9 %copy-start.11 = (u32[8]{0:T(128)S(1)}, u32[8]{0:T(128)}, u32[]{:S(2)}) copy-start(u32[8]{0:T(128)} %constant.45) | copy-start | bytes 100
  38.6 51.2 %copy-start.6 = (bf16[2048,128]{1,0:T(8,128)(2,1)S(1)}, bf16[2048,128]{1,0:T(8,128)(2,1)}, u32[]{:S(2)}) copy-start(bf16[2048,128]{1,0:T(8,128)(2,1)} %param.23) | copy-start | bytes 1572868
  38.6 59.3 %copy-start.7 = (bf16[2048,128]{1,0:T(8,128)(2,1)S(1)}, bf16[2048,128]{1,0:T(8,128)(2,1)}, u32[]{:S(2)}) copy-start(bf16[2048,128]{1,0:T(8,128)(2,1)} %param.24) | copy-start | bytes 1572868
  38.6 113.7 %all-gather.4.cloned.1.call-start = ((), (), s32[]{:S(2)}) async-start(), calls=%async_computation.4 | async-start | bytes 10485760 | tf_op jit(solution)/shard_map/all_gather | solution.py:67
  68.7 194.5 %reduce-scatter.3.cloned.1.call-start = ((), (), s32[]{:S(2)}) async-start(), calls=%async_computation.6 | async-start | bytes 786432 | tf_op jit(solution)/shard_map/reduce_scatter | solution.py:78
  152.3 99.1 %copy-start.9 = (bf16[2048]{0:T(1024)(128)(2,1)S(1)}, bf16[2048]{0:T(1024)(128)(2,1)}, u32[]{:S(2)}) copy-start(bf16[2048]{0:T(1024)(128)(2,1)} %param.26) | copy-start | bytes 12292
  152.3 110.8 %copy-start.4 = (bf16[32,2048]{1,0:T(8,128)(2,1)S(1)}, bf16[32,2048]{1,0:T(8,128)(2,1)}, u32[]{:S(2)}) copy-start(bf16[32,2048]{1,0:T(8,128)(2,1)} %param.16) | copy-start | bytes 393220
  251.4 60.6 %reduce-scatter.5.cloned.1.call-start = ((), (), s32[]{:S(2)}) async-start(), calls=%async_computation.7 | async-start | bytes 786432 | tf_op jit(solution)/shard_map/reduce_scatter | solution.py:84
  264.2 0.7 copy-start.5
  270.8 0.7 copy-start.2
  281.0 32.7 %copy-start.1 = (bf16[4096,256]{1,0:T(8,128)(2,1)S(1)}, bf16[4096,256]{1,0:T(8,128)(2,1)}, u32[]{:S(2)}) copy-start(bf16[4096,256]{1,0:T(8,128)(2,1)} %param.20) | copy-start | bytes 6291460
Sparse Core Ops, SparseCore 0:
  38.7 55.9 all-gather.5
  96.2 55.9 all-gather.3
  251.5 11.5 reduce-scatter.2
  300.2 11.7 reduce-scatter.4
where the time goes:
time: 321 us; the launch traced here: 320 us
  matrix products  101 us (31%)
  blocking collectives  94.4 us (29%)
  waiting for transfers between devices  69.3 us (22%)
  other arithmetic  33.8 us (11%)
  between operations  14.5 us (5%)
  local copies, waits for them, and re-layouts  6.94 us (2%)
    all_gather x1, waiting for transfers between devices, device_layer(): lax.all_gather(lax.all_to_all(cache_k, 'tp', 1, 0, tiled=True), 'cp', axi...  45.6 us
    dot_general x2, matrix products, attend_rows(): jnp.einsum('rkgd,skd->krgs', block_queries, cache_keys, preferred_element...  33 us
    dot_general x2, matrix products, attend_rows(): jnp.einsum('krgs,skd->krgd', cache_probs.astype(jnp.bfloat16), cache_valu...  31.1 us
    all_to_all x1, blocking collectives, device_layer(): lax.all_to_all(cache_v, 'tp', 1, 0, tiled=True)  30.2 us
    reduce_sum x2, other arithmetic, attend_rows(): jnp.sum(cache_probs, axis=-1, keepdims=True)  28.1 us
    all_to_all x1, blocking collectives, device_layer(): lax.all_to_all(cache_k, 'tp', 1, 0, tiled=True)  28 us
    dot_general x1, matrix products, device_layer(): mlp_part = jnp.dot(hidden_mlp, w_down, preferred_element_type=jnp.float32)  19 us
    reduce_scatter x1, waiting for transfers between devices, device_layer(): lax.psum_scatter(mlp_part, 'tp', scatter_dimension=0, tiled=True)  11.9 us
  transfers between devices with their start and end apart: 4, of which 3 were waited for; matrix products, arithmetic and copies ran while one was open for 3% of the time, Pallas kernels for 0%

commit v1 on v0

v1 whole, which is shorter than its diff:
```python
import functools
import math

import jax
import jax.numpy as jnp
from jax import lax
from jax.experimental import pallas as pl
from jax.experimental.pallas import tpu as pltpu
from jax.sharding import PartitionSpec as P

HEAD_DIM = 128
ROPE_BASE = 500000.0
NORM_EPS = 1e-5
MESH = pl.DeviceIdType.MESH
F32 = jnp.float32
BF16 = jnp.bfloat16

ROWS = 32
D = 2048
HEADS = 8
SLOTS = 8192
HALF = 4096
QT = ROWS * HEADS
CS = 1024
NCH = SLOTS // CS
SUB = 256
FCOLS = 2816
NEG = -(2.0 ** 100)
SCALE = math.log2(math.e) / math.sqrt(HEAD_DIM)
OROWS = HEAD_DIM + 8


def rel_position(index):
    dev, row = lax.div(index, ROWS), lax.rem(index, ROWS)
    half = ROWS // 2
    seg = jnp.where(row < half, dev, 15 - dev)
    return seg * half + lax.rem(row, half)


def rms(values, gain):
    inv = lax.rsqrt(jnp.mean(values * values, axis=-1, keepdims=True) + NORM_EPS)
    return (values * inv * gain).astype(BF16)


def kernel(len_ref, x_ref, cos_ref, sin_ref, g1_ref, g2_ref, ck_ref, cv_ref, wq_hbm, wk_hbm, wv_hbm, wo_hbm, wg_hbm, wu_hbm, wd_hbm,
           out_ref,
           wq, wk, wv, wo, wg, wu, wd, kbuf, vbuf, vt, bias, abuf, qown, qbuf, kvbuf, s0, s1, obuf, land, newo, hbuf, aout, asend, arecv,
           bbuf, ubuf, dsend, drecv, down, ysend, yrecv,
           ld_sem, cs_sem, cr_sem, a_sem, qs_sem, qr_sem, kvs_sem, kvr_sem, os_sem, or_sem, w_sem, bs_sem, br_sem,
           ds_sem, dr_sem, ys_sem, yr_sem):
    c = lax.axis_index('cp')
    t = lax.axis_index('tp')
    x, k = lax.div(c, 2), lax.rem(c, 2)
    xo, ko, to = 1 - x, 1 - k, 1 - t
    partner = {'cp': x * 2 + ko, 'tp': t}
    ynbr = {'cp': c, 'tp': to}
    is_worker = k == t

    def remote(src, dst, ssem, rsem, dev):
        return pltpu.make_async_remote_copy(src_ref=src, dst_ref=dst, send_sem=ssem, recv_sem=rsem, device_id=dev, device_id_type=MESH)

    barrier = pltpu.get_barrier_semaphore()
    for dc in range(4):
        for dt in range(2):
            if dc or dt:
                pl.semaphore_signal(barrier, inc=1, device_id={'cp': lax.rem(c + dc, 4), 'tp': lax.rem(t + dt, 2)}, device_id_type=MESH)

    def local(src, dst, i):
        return pltpu.make_async_copy(src, dst, ld_sem.at[i])

    kcol = pl.multiple_of(k * HEAD_DIM, HEAD_DIM)
    kocol = pl.multiple_of(ko * HEAD_DIM, HEAD_DIM)
    myhalf = pl.multiple_of(k * HALF, HALF)
    fcol = pl.multiple_of(k * (5504 - FCOLS), 128)
    l_wq = local(wq_hbm, wq, 0)
    l_wk = local(wk_hbm, wk, 1)
    l_wv = local(wv_hbm, wv, 2)
    l_k = local(ck_ref.at[:, pl.ds(kcol, HEAD_DIM)], kbuf.at[pl.ds(myhalf, HALF), :], 3)
    l_v = local(cv_ref.at[:, pl.ds(kcol, HEAD_DIM)], vbuf.at[pl.ds(myhalf, HALF), :], 4)
    l_wo = local(wo_hbm, wo, 5)
    l_wg = local(wg_hbm.at[:, pl.ds(fcol, FCOLS)], wg, 6)
    l_wu = local(wu_hbm.at[:, pl.ds(fcol, FCOLS)], wu, 7)
    l_wd = local(wd_hbm.at[pl.ds(fcol, FCOLS), :], wd, 8)
    for copy in (l_wq, l_wk, l_wv, l_v, l_k):
        copy.start()

    g1 = g1_ref[...].astype(F32)
    myrow = pl.multiple_of(t * ROWS, ROWS)
    abuf[pl.ds(myrow, ROWS), :] = rms(x_ref[...].astype(F32), g1)

    pl.semaphore_wait(barrier, 7)
    a_copy = remote(abuf.at[pl.ds(myrow, ROWS), :], abuf.at[pl.ds(myrow, ROWS), :], a_sem.at[0], a_sem.at[1], ynbr)
    a_copy.start()
    r_v = remote(cv_ref.at[:, pl.ds(kocol, HEAD_DIM)], vbuf.at[pl.ds(myhalf, HALF), :], cs_sem.at[0], cr_sem.at[0], partner)
    r_k = remote(ck_ref.at[:, pl.ds(kocol, HEAD_DIM)], kbuf.at[pl.ds(myhalf, HALF), :], cs_sem.at[1], cr_sem.at[1], partner)
    r_v.start()
    r_k.start()

    clen = len_ref[0]
    lane0 = lax.broadcasted_iota(jnp.int32, (SUB, HEAD_DIM), 1) == 0
    rowi = lax.broadcasted_iota(jnp.int32, (SUB, HEAD_DIM), 0)

    def bias_body(i, _):
        part = lax.div(i, HALF // SUB)
        base = HALF * (4 * x + 2 * part + t) + lax.rem(i, HALF // SUB) * SUB
        hidden = (rowi + base >= clen) & lane0
        bias[pl.ds(pl.multiple_of(i * SUB, SUB), SUB), :] = jnp.where(hidden, NEG, 0.0).astype(BF16)
        return 0

    lax.fori_loop(0, SLOTS // SUB, bias_body, 0)

    eye = (lax.broadcasted_iota(jnp.int32, (HEAD_DIM, HEAD_DIM), 0) == lax.broadcasted_iota(jnp.int32, (HEAD_DIM, HEAD_DIM), 1)).astype(F32).astype(BF16)

    def transpose_half(base):
        def body(i, _):
            off = pl.multiple_of(base + i * 512, 512)
            vals = vbuf[pl.ds(off, 512), :]
            vt[:, pl.ds(off, 512)] = lax.dot_general(eye, vals, (((1,), (1,)), ((), ())), preferred_element_type=F32).astype(BF16)
            return 0
        lax.fori_loop(0, HALF // 512, body, 0)

    l_v.wait()
    transpose_half(myhalf)

    l_wq.wait()
    l_wk.wait()
    l_wv.wait()
    for copy in (l_wo, l_wg, l_wu, l_wd):
        copy.start()
    a_copy.wait()
    acts = abuf[...]
    cos, sin = cos_ref[...], sin_ref[...]

    def rope(vals):
        return (vals * cos + pltpu.roll(vals, HEAD_DIM // 2, 1) * sin).astype(BF16)

    for hp in range(HEADS // 2):
        prod = jnp.dot(acts, wq[:, hp * 256:(hp + 1) * 256], preferred_element_type=F32)
        for sub in range(2):
            h = hp * 2 + sub
            rot = rope(prod[:, sub * HEAD_DIM:(sub + 1) * HEAD_DIM])
            qown[0, h * ROWS:(h + 1) * ROWS, :] = rot[:ROWS]
            qown[1, h * ROWS:(h + 1) * ROWS, :] = rot[ROWS:]

    def q_copy(dx, dy, ph):
        j = to if ph == 0 else t
        dev = {'cp': lax.rem(x + dx, 2) * 2 + t, 'tp': lax.rem(t + dy, 2)}
        n = (dx * 2 + dy) * 2 + ph
        return remote(qown.at[j], qbuf.at[c, j], qs_sem.at[n], qr_sem.at[c, j], dev)

    for ph in range(2):
        for dx, dy in ((0, 1), (0, 0), (1, 0), (1, 1)):
            if dx or dy:
                q_copy(dx, dy, ph).start()
            else:
                @pl.when(jnp.logical_not(is_worker))
                def _():
                    q_copy(0, 0, ph).start()

    @pl.when(is_worker)
    def _():
        qbuf[c] = qown[...]

    kvbuf[c, 0] = rope(jnp.dot(acts, wk[...], preferred_element_type=F32))
    kvbuf[c, 1] = jnp.dot(acts, wv[...], preferred_element_type=F32).astype(BF16)

    def kv_copy(dc):
        return remote(kvbuf.at[c], kvbuf.at[c], kvs_sem.at[dc], kvr_sem.at[c], {'cp': lax.rem(c + dc, 4), 'tp': t})

    for dc in range(1, 4):
        kv_copy(dc).start()

    cr_half = pl.multiple_of(ko * HALF, HALF)
    r_v.wait_recv()
    transpose_half(cr_half)
    l_k.wait()
    r_k.wait_recv()

    one_col = (lax.broadcasted_iota(jnp.int32, (QT, HEAD_DIM), 1) == 0).astype(F32).astype(BF16)

    def merge(ph):
        for dw in range(4):
            wx, wy = dw // 2, dw % 2
            slot = lax.rem(x + wx, 2) * 2 + lax.rem(t + wy, 2)
            recv = remote(obuf.at[0], land.at[ph, slot], os_sem.at[0], or_sem.at[ph, slot], ynbr)
            if dw == 0:
                @pl.when(jnp.logical_not(is_worker))
                def _():
                    recv.wait_recv()
            else:
                recv.wait_recv()
        parts = [land[ph, w] for w in range(4)] + [newo[ph]]
        tops = [p[HEAD_DIM:HEAD_DIM + 1] for p in parts]
        top = functools.reduce(jnp.maximum, tops)
        scales = [jnp.exp2((m - top) * SCALE) for m in tops]
        total = sum(s * p[HEAD_DIM + 1:HEAD_DIM + 2] for s, p in zip(scales, parts))
        mixed = sum(s * p[:HEAD_DIM] for s, p in zip(scales, parts)) / total
        turned = mixed.T.astype(BF16)
        for h in range(HEADS):
            aout[:, h * HEAD_DIM:(h + 1) * HEAD_DIM] = turned[h * ROWS:(h + 1) * ROWS]
        return aout[...]

    def out_product(ph, store):
        vals = merge(ph)

        def body(i, _):
            cols = pl.ds(pl.multiple_of(i * 512, 512), 512)
            store(cols, jnp.dot(vals, wo[:, cols], preferred_element_type=F32))
            return 0
        lax.fori_loop(0, D // 512, body, 0)

    w_copy = remote(asend, arecv, w_sem.at[0], w_sem.at[1], ynbr)

    def new_rows():
        for dc in range(1, 4):
            src = lax.rem(c + dc, 4)
            remote(kvbuf.at[src], kvbuf.at[src], kvs_sem.at[0], kvr_sem.at[src], ynbr).wait_recv()
        keys = jnp.concatenate([kvbuf[b, 0] for b in range(4)], axis=0)
        vals = jnp.concatenate([kvbuf[b, 1] for b in range(4)], axis=0)
        key_pos = rel_position(lax.broadcasted_iota(jnp.int32, (256, QT), 0))
        lane = lax.rem(lax.broadcasted_iota(jnp.int32, (256, QT), 1), ROWS)
        for ph in range(2):
            j = to if ph == 0 else t
            scores = lax.dot_general(keys, qown[j], (((1,), (1,)), ((), ())), preferred_element_type=F32)
            scores = jnp.where(key_pos <= rel_position((c * 2 + j) * ROWS + lane), scores, NEG)
            top = jnp.max(scores, axis=0, keepdims=True)
            probs = jnp.exp2((scores - top) * SCALE)
            newo[ph, :HEAD_DIM, :] = lax.dot_general(vals, probs.astype(BF16), (((0,), (0,)), ((), ())), preferred_element_type=F32)
            newo[ph, HEAD_DIM:HEAD_DIM + 1, :] = top
            newo[ph, HEAD_DIM + 1:HEAD_DIM + 2, :] = jnp.sum(probs, axis=0, keepdims=True)

    def tile_place(n):
        ph, i = lax.div(n, 4), lax.rem(n, 4)
        flip = lax.rem(ph + lax.div(i, 2), 2)
        dk = lax.rem(ph + i, 2)
        blk = lax.rem(x + flip, 2) * 2 + lax.rem(k + dk, 2)
        j = lax.rem(k + 1 + ph, 2)
        return ph, blk, j

    def o_copy(n):
        ph, blk, _ = tile_place(n)
        slot = x * 2 + t
        return remote(obuf.at[n], land.at[ph, slot], os_sem.at[n], or_sem.at[ph, slot], {'cp': blk, 'tp': k})

    def scores_of(qa, ci, s_ref):
        top = None
        for sub in range(CS // SUB):
            rows = pl.ds(pl.multiple_of(ci * CS + sub * SUB, SUB), SUB)
            ka = jnp.concatenate([kbuf[rows, :], bias[rows, :]], axis=1)
            s = lax.dot_general(ka, qa, (((1,), (1,)), ((), ())), preferred_element_type=F32)
            s_ref[sub * SUB:(sub + 1) * SUB, :] = s
            mx = jnp.max(s.reshape(SUB // 8, 8, QT), axis=0)
            top = mx if top is None else jnp.maximum(top, mx)
        return jnp.max(top, axis=0, keepdims=True)

    def absorb(ci, s_ref, m_new, m, l, o):
        alpha = jnp.exp2((m - m_new) * SCALE)
        l = l * alpha
        acc = None
        for sub in range(CS // SUB):
            p = jnp.exp2((s_ref[sub * SUB:(sub + 1) * SUB, :] - m_new) * SCALE)
            l = l + jnp.sum(p.reshape(SUB // 8, 8, QT), axis=0)
            cols = pl.ds(pl.multiple_of(ci * CS + sub * SUB, SUB), SUB)
            part = jnp.dot(vt[:, cols], p.astype(BF16), preferred_element_type=F32)
            acc = part if acc is None else acc + part
        return l, o * alpha + acc

    def tile_body(n, _):
        ph, blk, j = tile_place(n)
        mine = jnp.logical_and(is_worker, blk == c)

        @pl.when(jnp.logical_not(mine))
        def _():
            remote(qown.at[j], qbuf.at[blk, j], qs_sem.at[0], qr_sem.at[blk, j], ynbr).wait_recv()

        @pl.when(n == 6)
        def _():
            new_rows()
            l_wo.wait()

            def store(cols, vals):
                asend[:, cols] = vals
            out_product(0, store)
            w_copy.start()

        qa = jnp.concatenate([qbuf[blk, j], one_col], axis=1)
        m0 = scores_of(qa, 0, s0)
        m = m0
        l = jnp.zeros((8, QT), F32)
        o = jnp.zeros((HEAD_DIM, QT), F32)

        def pair(i, carry):
            m, m0, l, o = carry
            m1 = jnp.maximum(m0, scores_of(qa, 2 * i + 1, s1))
            l, o = absorb(2 * i, s0, m0, m, l, o)
            nxt = jnp.minimum(2 * i + 2, NCH - 1)
            m2 = jnp.maximum(m1, scores_of(qa, nxt, s0))
            l, o = absorb(2 * i + 1, s1, m1, m0, l, o)
            return m1, m2, l, o

        m, _, l, o = lax.fori_loop(0, NCH // 2, pair, (m, m0, l, o))
        obuf[n, :HEAD_DIM, :] = o
        obuf[n, HEAD_DIM:HEAD_DIM + 1, :] = m
        obuf[n, HEAD_DIM + 1:HEAD_DIM + 2, :] = jnp.sum(l, axis=0, keepdims=True)

        @pl.when(jnp.logical_not(mine))
        def _():
            o_copy(n).start()

        @pl.when(mine)
        def _():
            land[ph, x * 2 + t] = obuf[n]
        return 0

    lax.fori_loop(0, 8, tile_body, 0)

    def store_mid(cols, vals):
        hbuf[:, cols] = vals
    out_product(1, store_mid)
    w_copy.wait_recv()
    mid = (x_ref[...].astype(F32) + (hbuf[...] + arecv[...])).astype(BF16)
    hbuf[...] = mid.astype(F32)

    place = pl.multiple_of((k * 2 + t) * ROWS, ROWS)
    bbuf[pl.ds(place, ROWS), :] = rms(mid.astype(F32), g2_ref[...].astype(F32))
    hr = ROWS // 2

    def b_copy(kind, i):
        if kind == 0:
            rows, dev = pl.multiple_of(place + i * hr, hr), ynbr
        elif kind == 1:
            rows, dev = pl.multiple_of(place + i * hr, hr), partner
        else:
            rows, dev = pl.multiple_of((k * 2 + to) * ROWS + i * hr, hr), partner
        piece = bbuf.at[pl.ds(rows, hr), :]
        return remote(piece, piece, bs_sem.at[kind, i], br_sem.at[kind, i], dev)

    for kind in (0, 1):
        for i in range(2):
            b_copy(kind, i).start()
    for i in range(2):
        b_copy(0, i).wait_recv()
        b_copy(2, i).start()
    l_wg.wait()
    l_wu.wait()
    for i in range(2):
        b_copy(1, i).wait_recv()
    for i in range(2):
        b_copy(2, i).wait_recv()

    def mlp_body(i, _):
        cols = pl.ds(pl.multiple_of(i * 256, 256), 256)
        acts2 = bbuf[...]
        gate = jnp.dot(acts2, wg[:, cols], preferred_element_type=F32)
        up = jnp.dot(acts2, wu[:, cols], preferred_element_type=F32)
        vals = gate / (1.0 + jnp.exp(-gate)) * up
        col = lax.broadcasted_iota(jnp.int32, (4 * ROWS, 256), 1) + i * 256
        keep = col >= k * (2 * FCOLS - 5504)
        ubuf[:, cols] = jnp.where(keep, vals, 0.0).astype(BF16)
        return 0

    lax.fori_loop(0, FCOLS // 256, mlp_body, 0)
    l_wd.wait()

    def d_copy(n):
        return remote(dsend.at[n], drecv.at[n], ds_sem.at[n], dr_sem.at[n], partner)

    def y_copy(n):
        return remote(ysend.at[n], yrecv.at[n], ys_sem.at[n], yr_sem.at[n], ynbr)

    keep_rows = pl.multiple_of(k * 64, 64)
    give_rows = pl.multiple_of(ko * 64, 64)

    def pass_on(n):
        d_copy(n).wait_recv()
        ysend[n] = down[n, pl.ds(keep_rows + pl.multiple_of(to * ROWS, ROWS), ROWS), :] + drecv[n, pl.ds(pl.multiple_of(to * ROWS, ROWS), ROWS), :]
        y_copy(n).start()

    lag = 4
    nblk = D // 256
    for n in range(nblk + lag):
        if n < nblk:
            down[n] = jnp.dot(ubuf[...], wd[:, n * 256:(n + 1) * 256], preferred_element_type=F32)
            dsend[n] = down[n, pl.ds(give_rows, 64), :]
            d_copy(n).start()
        if n >= lag:
            pass_on(n - lag)
    for n in range(nblk):
        y_copy(n).wait_recv()
        own = down[n, pl.ds(keep_rows + myrow, ROWS), :] + drecv[n, pl.ds(myrow, ROWS), :]
        cols = slice(n * 256, (n + 1) * 256)
        out_ref[:, cols] = (hbuf[:, cols] + (own + yrecv[n])).astype(BF16)

    r_v.wait_send()
    r_k.wait_send()
    for ph in range(2):
        for dx, dy in ((0, 1), (0, 0), (1, 0), (1, 1)):
            if dx or dy:
                q_copy(dx, dy, ph).wait_send()
            else:
                @pl.when(jnp.logical_not(is_worker))
                def _():
                    q_copy(0, 0, ph).wait_send()
    for dc in range(1, 4):
        kv_copy(dc).wait_send()

    def drain(n, _):
        _, blk, _ = tile_place(n)

        @pl.when(jnp.logical_not(jnp.logical_and(is_worker, blk == c)))
        def _():
            o_copy(n).wait_send()
        return 0

    lax.fori_loop(0, 8, drain, 0)
    w_copy.wait_send()
    for kind in range(3):
        for i in range(2):
            b_copy(kind, i).wait_send()
    for n in range(nblk):
        d_copy(n).wait_send()
        y_copy(n).wait_send()


def solution(mesh):
    token_spec = P(('dp', 'cp', 'tp'), None)
    column_spec = P(None, 'tp')
    row_spec = P('tp', None)

    def device_layer(hidden_loc, pos_loc, cache_len, cache_k, cache_v, norm1_gain, w_query, w_key, w_value, w_out, norm2_gain, w_gate, w_up, w_down):
        c = lax.axis_index('cp')
        pos = cache_len[0] + rel_position(c * 64 + jnp.arange(64, dtype=jnp.int32))
        half_dim = HEAD_DIM // 2
        inv_freq = 1.0 / (ROPE_BASE ** (jnp.arange(half_dim, dtype=F32) * (2.0 / HEAD_DIM)))
        angles = pos.astype(F32)[:, None] * inv_freq[None, :]
        cos, sin = jnp.cos(angles), jnp.sin(angles)
        cos2 = jnp.concatenate([cos, cos], axis=1)
        sin2 = jnp.concatenate([-sin, sin], axis=1)
        vmem = pl.BlockSpec(memory_space=pltpu.VMEM)
        hbm = pl.BlockSpec(memory_space=pl.ANY)
        dma = pltpu.SemaphoreType.DMA
        return pl.pallas_call(
            kernel,
            out_shape=jax.ShapeDtypeStruct((ROWS, D), BF16),
            in_specs=[pl.BlockSpec(memory_space=pltpu.SMEM)] + [vmem] * 5 + [hbm] * 9,
            out_specs=vmem,
            scratch_shapes=[
                pltpu.VMEM((D, 1024), BF16), pltpu.VMEM((D, 128), BF16), pltpu.VMEM((D, 128), BF16), pltpu.VMEM((1024, D), BF16),
                pltpu.VMEM((D, FCOLS), BF16), pltpu.VMEM((D, FCOLS), BF16), pltpu.VMEM((FCOLS, D), BF16),
                pltpu.VMEM((SLOTS, HEAD_DIM), BF16), pltpu.VMEM((SLOTS, HEAD_DIM), BF16), pltpu.VMEM((HEAD_DIM, SLOTS), BF16),
                pltpu.VMEM((SLOTS, HEAD_DIM), BF16),
                pltpu.VMEM((2 * ROWS, D), BF16), pltpu.VMEM((2, QT, HEAD_DIM), BF16), pltpu.VMEM((4, 2, QT, HEAD_DIM), BF16),
                pltpu.VMEM((4, 2, 64, HEAD_DIM), BF16),
                pltpu.VMEM((CS, QT), F32), pltpu.VMEM((CS, QT), F32),
                pltpu.VMEM((8, OROWS, QT), F32), pltpu.VMEM((2, 4, OROWS, QT), F32), pltpu.VMEM((2, OROWS, QT), F32),
                pltpu.VMEM((ROWS, D), F32), pltpu.VMEM((ROWS, 1024), BF16), pltpu.VMEM((ROWS, D), F32), pltpu.VMEM((ROWS, D), F32),
                pltpu.VMEM((4 * ROWS, D), BF16), pltpu.VMEM((4 * ROWS, FCOLS), BF16),
                pltpu.VMEM((8, 64, 256), F32), pltpu.VMEM((8, 64, 256), F32), pltpu.VMEM((8, 128, 256), F32),
                pltpu.VMEM((8, ROWS, 256), F32), pltpu.VMEM((8, ROWS, 256), F32),
                dma((9,)), dma((2,)), dma((2,)), dma((2,)), dma((8,)), dma((4, 2)), dma((4,)), dma((4,)), dma((8,)), dma((2, 4)), dma((2,)),
                dma((3, 2)), dma((3, 2)), dma((8,)), dma((8,)), dma((8,)), dma((8,)),
            ],
            compiler_params=pltpu.CompilerParams(collective_id=0, has_side_effects=True, vmem_limit_bytes=67043328),
            name='layer',
        )(cache_len, hidden_loc, cos2, sin2, norm1_gain.reshape(1, D), norm2_gain.reshape(1, D), cache_k, cache_v,
          w_query, w_key, w_value, w_out, w_gate, w_up, w_down)

    return jax.shard_map(device_layer, mesh=mesh, in_specs=(token_spec, P(('dp', 'cp', 'tp')), P('dp'), token_spec, token_spec, P(), column_spec, column_spec, column_spec, row_spec, P(), column_spec, column_spec, row_spec), out_specs=token_spec, check_vma=False)
```

time: 321 us -> 81.8 us (0.25)
  matrix products: 101 us -> 0 us
  blocking collectives: 94.4 us -> 0 us
  Pallas kernels: 0 us -> 75.9 us
  waiting for transfers between devices: 69.3 us -> 0 us
  other arithmetic: 33.8 us -> 0.93 us
  between operations: 14.5 us -> 0.67 us
    dot_general x14 -> x0, matrix products: 101 us -> none  [the longest x2 33 us: attend_rows(): jnp.einsum('rkgd,skd->krgs', block_queries, cache_keys, preferred_element...]
    pallas_call x0 -> x1, Pallas kernels: none -> 75.9 us  [device_layer(): pl.pallas_call(kernel, out_shape=jax.ShapeDtypeStruct((ROWS, D), BF16), i...]
    all_to_all x2 -> x0, blocking collectives: 58.2 us -> none  [the longest x1 30.2 us: device_layer(): lax.all_to_all(cache_v, 'tp', 1, 0, tiled=True)]
    all_gather x2 -> x0, waiting for transfers between devices: 45.6 us -> none  [the longest x1 45.6 us: device_layer(): lax.all_gather(lax.all_to_all(cache_k, 'tp', 1, 0, tiled=True), 'cp', axi...]
    reduce_sum x6 -> x0, other arithmetic: 29.7 us -> none  [the longest x2 28.1 us: attend_rows(): jnp.sum(cache_probs, axis=-1, keepdims=True)]
    all_gather x4 -> x0, blocking collectives: 27.1 us -> none  [the longest x1 8.1 us: device_layer(): new_values = lax.all_gather(values_loc, 'cp', axis=0, tiled=True)]
    reduce_scatter x2 -> x0, waiting for transfers between devices: 23.6 us -> none  [the longest x1 11.9 us: device_layer(): lax.psum_scatter(mlp_part, 'tp', scatter_dimension=0, tiled=True)]
    unnamed x2 -> x0, blocking collectives: 9.13 us -> none
  transfers between devices with their start and end apart: 4 -> 0, of which waited for: 3 -> 0; matrix products, arithmetic and copies ran while one was open for 3% -> 0% of each run, Pallas kernels for 0% -> 0%
where the time goes in v1:
time: 81.8 us; the launch traced here: 81.6 us
  Pallas kernels  75.9 us (93%)
  local copies, waits for them, and re-layouts  4.14 us (5%)
  other arithmetic  0.93 us (1%)
    pallas_call x1, Pallas kernels, device_layer(): pl.pallas_call(kernel, out_shape=jax.ShapeDtypeStruct((ROWS, D), BF16), i...  75.9 us

profile of v1, /device:TPU:0, one launch (start us, length us, event | category | flops | bytes accessed | tf_op | source)
XLA Modules:
  0.0 81.6 jit_solution(16519158346776318956)
XLA Ops:
  0.7 1.3 %reshape.38.g1_ref = bf16[1,2048]{1,0:T(2,128)(2,1)} reshape(bf16[2048]{0:T(1024)(128)(2,1)} %param.18) | data formatting | bytes 8192 | tf_op jit(solution)/shard_map/reshape | solution.py:465
  2.0 1.3 %reshape.39.g2_ref = bf16[1,2048]{1,0:T(2,128)(2,1)} reshape(bf16[2048]{0:T(1024)(128)(2,1)} %param.23) | data formatting | bytes 8192 | tf_op jit(solution)/shard_map/reshape | solution.py:465
  3.3 0.2 fusion
  3.5 0.7 pad_maximum_fusion
  4.2 75.9 %layer.1 = bf16[32,2048]{1,0:T(8,128)(2,1)} custom-call(s32[1]{0:T(128)} %copy.15.len_ref, bf16[32,2048]{1,0:T(8,128)(2,1)} %x_ref.1, f32[64,128]{1,0:T(8,128)} %get-tuple-element.8.cos_ref, f32[64,128]{1,0:T(8,128)} %get-tuple-element.9.sin_ref, bf16[1,2048]{1,0:T(2,128)(2,1)} %reshape.38.g1_ref, bf16[1,2048]{1,0:T(2,128)(2,1)} %reshape.39.g2_ref, ...), custom_call_target="tpu_custom_call" | custom-call | tf_op jit(solution)/shard_map/layer/pallas_call | solution.py:442
  80.0 1.6 %copy.16 = bf16[32,2048]{1,0:T(8,128)(2,1)} copy(bf16[32,2048]{1,0:T(8,128)(2,1)} %layer.1) | data formatting | bytes 262144
  (2 shorter events, 0.0 us)

commit v2 on v0

v2 whole, which is shorter than its diff:
```python
import functools
import math
import operator

import jax
import jax.numpy as jnp
from jax import lax
from jax.experimental import pallas as pl
from jax.experimental.pallas import tpu as pltpu
from jax.sharding import PartitionSpec as P

HEAD_DIM = 128
ROPE_BASE = 500000.0
NORM_EPS = 1e-5
MESH = pl.DeviceIdType.MESH
F32 = jnp.float32
BF16 = jnp.bfloat16

ROWS = 32
D = 2048
HEADS = 8
SLOTS = 8192
HALF = 4096
QT = ROWS * HEADS
CS = 1024
NCH = SLOTS // CS
VT = 512
ASIDE = 6
KC = 512
NC = 512
PART = 512
FCOLS = 2816
NEG = -(2.0 ** 100)
SCALE = math.log2(math.e) / math.sqrt(HEAD_DIM)
OROWS = HEAD_DIM + 8
PAIR = range(2)
OUT, TOP, NORM = (slice(*b) for b in ((0, HEAD_DIM), (HEAD_DIM, HEAD_DIM + 1), (HEAD_DIM + 1, HEAD_DIM + 2)))
CONTRACT_LAST = (((1,), (1,)), ((), ()))
PI_A = 201.0 / 128.0
PI_B = round((math.pi / 2 - PI_A) * 2.0 ** 20) / 2.0 ** 20
PI_C = math.pi / 2 - PI_A - PI_B


def rel_position(index):
    half = ROWS // 2
    dev, high = index >> 5, (index >> 4) & 1
    seg = dev + high * (15 - 2 * dev)
    return seg * half + (index & (half - 1))


def turn(angle):
    n = jnp.floor(angle * (2.0 / math.pi) + 0.5)
    r = ((angle - n * PI_A) - n * PI_B) - n * PI_C
    z = r * r
    sin = r + r * z * (-1.6666654611e-1 + z * (8.3321608736e-3 + z * -1.9515295891e-4))
    cos = 1.0 - 0.5 * z + z * z * (4.166664568298827e-2 + z * (-1.388731625493765e-3 + z * 2.443315711809948e-5))
    quarter = n - 4.0 * jnp.floor(n * 0.25)
    odd = (quarter == 1.0) | (quarter == 3.0)
    cos, sin = jnp.where(odd, sin, cos), jnp.where(odd, cos, sin)
    return jnp.where((quarter == 1.0) | (quarter == 2.0), -cos, cos), jnp.where(quarter >= 2.0, -sin, sin)


def par(first, *more):
    return lax.rem(sum(more, first), 2)


def over_rows(op, vals):
    return op(vals, axis=0, keepdims=True)


def block(i, size):
    return slice(i * size, (i + 1) * size)


def wide(gain_ref):
    gain = gain_ref[...].astype(F32)
    return jnp.concatenate([gain[i:i + 1] for i in range(D // 128)], axis=1)


def rms(values, gain):
    inv = lax.rsqrt(jnp.mean(values * values, axis=-1, keepdims=True) + NORM_EPS)
    return (values * inv * gain).astype(BF16)


def kernel(len_ref, x_hbm, freq_hbm, g1_hbm, g2_hbm, ck_ref, cv_ref, wq_hbm, wk_hbm, wv_hbm, wo_hbm, wg_hbm, wu_hbm, wd_hbm,
           out_hbm,
           x_ref, freq_ref, g1_ref, g2_ref, wq, wk, wv, wo, wg, wu, wd, kbuf, vbuf, vt, abuf, qown, qbuf, kvbuf, s0, s1, p0, p1, oacc, obuf, passing, land, newo, hbuf, asend, arecv,
           bbuf, ubuf, drecv, yrecv, out_ref,
           ld_sem, cs_sem, cr_sem, a_sem, qs_sem, qr_sem, kvs_sem, kvr_sem, os_sem, ps_sem, or_sem, ws_sem, wr_sem, bs_sem, br_sem,
           us_sem, ur_sem, ds_sem, dr_sem, ys_sem, yr_sem, out_sem):
    c = lax.axis_index('cp')
    t = lax.axis_index('tp')
    x, k = lax.div(c, 2), par(c)
    xo, ko, to = 1 - x, 1 - k, 1 - t
    partner = {'cp': x * 2 + ko, 'tp': t}
    ynbr = {'cp': c, 'tp': to}
    is_worker = k == t

    def remote(src, dst, ssem, rsem, dev):
        return pltpu.make_async_remote_copy(src_ref=src, dst_ref=dst, send_sem=ssem, recv_sem=rsem, device_id=dev, device_id_type=MESH)

    barrier = pltpu.get_barrier_semaphore()
    for dc in range(4):
        for dt in PAIR:
            if dc or dt:
                pl.semaphore_signal(barrier, inc=1, device_id={'cp': lax.rem(c + dc, 4), 'tp': par(t, dt)}, device_id_type=MESH)

    def local(src, dst, i):
        return pltpu.make_async_copy(src, dst, ld_sem.at[i])

    kcol = pl.multiple_of(k * HEAD_DIM, HEAD_DIM)
    kocol = pl.multiple_of(ko * HEAD_DIM, HEAD_DIM)
    myhalf = pl.multiple_of(k * HALF, HALF)
    fcol = pl.multiple_of(k * (5504 - FCOLS), 128)
    l_wq = local(wq_hbm, wq, 0)
    l_wk = local(wk_hbm, wk, 1)
    l_wv = local(wv_hbm, wv, 2)
    l_k = local(ck_ref.at[:, pl.ds(kcol, HEAD_DIM)], kbuf.at[pl.ds(myhalf, HALF), :], 3)
    l_v = local(cv_ref.at[:, pl.ds(kcol, HEAD_DIM)], vbuf.at[pl.ds(myhalf, HALF), :], 4)
    l_wo = local(wo_hbm, wo, 5)
    l_wg = local(wg_hbm.at[:, pl.ds(fcol, FCOLS)], wg, 6)
    l_wu = local(wu_hbm.at[:, pl.ds(fcol, FCOLS)], wu, 7)
    l_wd = local(wd_hbm.at[:, pl.ds(pl.multiple_of(k * (D // 2), 128), D // 2)], wd, 8)
    l_x = local(x_hbm, x_ref, 9)
    l_g1 = local(g1_hbm, g1_ref, 10)
    l_g2 = local(g2_hbm, g2_ref, 11)
    l_freq = local(freq_hbm, freq_ref, 12)
    for copy in (l_x, l_g1, l_wq, l_v, l_wk, l_wv, l_freq, l_k, l_g2):
        copy.start()

    l_x.wait()
    l_g1.wait()
    g1 = wide(g1_ref)
    myrow = pl.multiple_of(t * ROWS, ROWS)
    abuf[pl.ds(myrow, ROWS), :] = rms(x_ref[...].astype(F32), g1)

    pl.semaphore_wait(barrier, 7)
    a_copy = remote(abuf.at[pl.ds(myrow, ROWS), :], abuf.at[pl.ds(myrow, ROWS), :], a_sem.at[0], a_sem.at[1], ynbr)
    a_copy.start()
    r_v = remote(cv_ref.at[:, pl.ds(kocol, HEAD_DIM)], vbuf.at[pl.ds(myhalf, HALF), :], cs_sem.at[0], cr_sem.at[0], partner)
    r_k = remote(ck_ref.at[:, pl.ds(kocol, HEAD_DIM)], kbuf.at[pl.ds(myhalf, HALF), :], cs_sem.at[1], cr_sem.at[1], partner)
    r_v.start()
    r_k.start()

    clen = len_ref[0]
    rowi, lane = (lax.broadcasted_iota(jnp.int32, (VT, HEAD_DIM), i) for i in PAIR)
    lane0 = lane == 0
    eye = operator.eq(*(lax.broadcasted_iota(jnp.int32, (HEAD_DIM, HEAD_DIM), i) for i in PAIR)).astype(F32).astype(BF16)

    def turn_half(core):
        def body(i, _):
            off = pl.multiple_of(core * HALF + i * VT, VT)
            vals = vbuf[pl.ds(off, VT), :]
            vt[:, pl.ds(off, VT)] = lax.dot_general(eye, vals, CONTRACT_LAST, preferred_element_type=F32).astype(BF16)
            hidden = (rowi + (HALF * (4 * x + 2 * core + t) + i * VT) >= clen) & lane0
            vbuf[pl.ds(off, VT), :] = jnp.where(hidden, NEG, 0.0).astype(BF16)
            return 0
        lax.fori_loop(0, HALF // VT, body, 0)

    l_v.wait()
    turn_half(k)

    one_col = (lax.broadcasted_iota(jnp.int32, (QT, HEAD_DIM), 1) == 0).astype(F32).astype(BF16)
    for n in range(8):
        qbuf[n, :, HEAD_DIM:] = one_col
    l_freq.wait()
    pos = clen + rel_position(c * 64 + lax.broadcasted_iota(jnp.int32, (64, HEAD_DIM // 2), 0))
    cos, sin = turn(pos.astype(F32) * freq_ref[0:1, :])
    oacc[...] = jnp.zeros((HEAD_DIM, QT), F32)

    l_wq.wait()
    l_wk.wait()
    l_wv.wait()
    for copy in (l_wo, l_wg, l_wu, l_wd):
        copy.start()
    a_copy.wait()
    acts = abuf[...]
    cos = jnp.concatenate([cos, cos], axis=1)
    sin = jnp.concatenate([-sin, sin], axis=1)

    def rope(vals):
        return (vals * cos + pltpu.roll(vals, HEAD_DIM // 2, 1) * sin).astype(BF16)

    for hp in range(HEADS // 2):
        prod = jnp.dot(acts, wq[:, hp * 256:(hp + 1) * 256], preferred_element_type=F32)
        for sub in PAIR:
            h = hp * 2 + sub
            rot = rope(prod[:, sub * HEAD_DIM:(sub + 1) * HEAD_DIM])
            qown[0, h * ROWS:(h + 1) * ROWS, :] = rot[:ROWS]
            qown[1, h * ROWS:(h + 1) * ROWS, :] = rot[ROWS:]

    def q_copy(dx, dy, ph):
        j = to if ph == 0 else t
        dev = {'cp': par(x, dx) * 2 + t, 'tp': par(t, dy)}
        n = (dx * 2 + dy) * 2 + ph
        tile = ph * 4 + (dx + max(dy, ph)) % 2 * 2 + par(k, t, ph)
        return remote(qown.at[j], qbuf.at[tile, :, :HEAD_DIM], qs_sem.at[n], qr_sem.at[tile], dev)

    def send_queries(ph, places):
        for dx, dy in places:
            if dx or dy:
                q_copy(dx, dy, ph).start()
            else:
                @pl.when(jnp.logical_not(is_worker))
                def _():
                    q_copy(0, 0, ph).start()

    send_queries(0, ((1, 1), (0, 0)))

    @pl.when(is_worker)
    def _():
        qbuf[0, :, :HEAD_DIM] = qown[to]
        qbuf[7, :, :HEAD_DIM] = qown[t]

    kvbuf[c, 0] = rope(jnp.dot(acts, wk[...], preferred_element_type=F32))
    kvbuf[c, 1] = jnp.dot(acts, wv[...], preferred_element_type=F32).astype(BF16)

    def kv_copy(dc):
        return remote(kvbuf.at[c], kvbuf.at[c], kvs_sem.at[dc], kvr_sem.at[c], {'cp': lax.rem(c + dc, 4), 'tp': t})

    r_v.wait_recv()
    turn_half(ko)
    send_queries(0, ((0, 1), (1, 0)))
    l_k.wait()
    r_k.wait_recv()

    nblk = D // NC

    def wait_parts(group, first):
        for slot in range(first, 3):
            recv = remote(obuf.at[0], land.at[group, slot], os_sem.at[0], or_sem.at[group, slot], ynbr)
            if slot:
                recv.wait_recv()
            else:
                pl.when(jnp.logical_not(is_worker))(recv.wait_recv)

    def merge(group):
        parts = [land[group, w] for w in range(3)] + [newo[group]]
        tops = [p[TOP] for p in parts]
        top = functools.reduce(jnp.maximum, tops)
        scales = [jnp.exp2((m - top) * SCALE) for m in tops]
        total = sum(s * p[NORM] for s, p in zip(scales, parts))
        mixed = sum(s * p[OUT] for s, p in zip(scales, parts)) / total
        turned = mixed.T.astype(BF16)
        return jnp.concatenate([turned[block(h, ROWS)] for h in range(HEADS)], axis=1)

    def w_copy(e, i):
        piece = asend.at[i, pl.ds(pl.multiple_of(e * ROWS, ROWS), ROWS)]
        return remote(piece, arecv.at[i], ws_sem.at[e, i], wr_sem.at[i], {'cp': x * 2 + e, 'tp': to})

    def wait_new():
        for dc in range(1, 4):
            src = lax.rem(c + dc, 4)
            remote(kvbuf.at[src], kvbuf.at[src], kvs_sem.at[0], kvr_sem.at[src], ynbr).wait_recv()

    def new_rows(group, query, dev):
        keys = jnp.concatenate([kvbuf[b, 0] for b in range(4)], axis=0)
        vals = jnp.concatenate([kvbuf[b, 1] for b in range(4)], axis=0)
        key_pos = rel_position(lax.broadcasted_iota(jnp.int32, (256, QT), 0))
        lane = lax.broadcasted_iota(jnp.int32, (1, QT), 1) & (ROWS - 1)
        scores = lax.dot_general(keys, query, CONTRACT_LAST, preferred_element_type=F32)
        scores = jnp.where(key_pos <= rel_position(dev * ROWS + lane), scores, NEG)
        top = over_rows(jnp.max, scores)
        probs = jnp.exp2((scores - top) * SCALE)
        newo[group, OUT, :] = lax.dot_general(vals, probs.astype(BF16), (((0,), (0,)), ((), ())), preferred_element_type=F32)
        newo[group, TOP, :] = top
        newo[group, NORM, :] = over_rows(jnp.sum, probs)

    def tile_place(n):
        ph, i = lax.div(n, 4), lax.rem(n, 4)
        flip = par(jnp.maximum(ph, par(k, t)), lax.div(i, 2))
        dk = par(ph, i)
        blk = par(x, flip) * 2 + par(k, dk)
        j = par(k, 1, ph)
        return ph, blk, j, flip

    def o_copy(n):
        ph, blk, _, flip = tile_place(n)
        group = jnp.where(ph == 1, 2, par(blk))
        slot = jnp.where(is_worker, flip, 2)
        dev = jnp.where(ph == 1, blk, lax.div(blk, 2) * 2 + k)
        return remote(obuf.at[n + 1], land.at[group, slot], os_sem.at[n], or_sem.at[group, slot], {'cp': dev, 'tp': k})

    def stays(n):
        ph, blk, _, flip = tile_place(n)
        return jnp.logical_and(is_worker, jnp.where(ph == 1, blk == c, flip == 0))

    def goes(n):
        return jnp.logical_and(is_worker, jnp.logical_not(stays(n)))

    def far_copy(n):
        spot = lax.div(n, 4) * 2 + par(n)
        return remote(obuf.at[n + 1], passing.at[spot], os_sem.at[n], ps_sem.at[spot], {'cp': xo * 2 + k, 'tp': t})

    def wait_query(n):
        @pl.when(jnp.logical_not(jnp.logical_and(is_worker, lax.rem(n, 7) == 0)))
        def _():
            remote(qown.at[0], qbuf.at[n, :, :HEAD_DIM], qs_sem.at[0], qr_sem.at[n], ynbr).wait_recv()

    def part_rows(part):
        return slice(part * PART, (part + 1) * PART)

    def part_slots(ci, part):
        return slice(ci * CS + part * PART, ci * CS + (part + 1) * PART)

    def scores_of(qa, ci, part, top, s_ref):
        rows = part_slots(ci, part)
        ka = jnp.concatenate([kbuf[rows, :], vbuf[rows, :]], axis=1)
        s = lax.dot_general(ka, qa, CONTRACT_LAST, preferred_element_type=F32)
        s_ref[part_rows(part), :] = s
        mx = jnp.max(s.reshape(PART // 8, 8, QT), axis=0)
        return mx if top is None else jnp.maximum(top, mx)

    def probs_of(part, m, l, s_ref, p_ref):
        p = jnp.exp2((s_ref[part_rows(part), :] - m) * SCALE)
        p_ref[part_rows(part), :] = p.astype(BF16)
        return l + jnp.sum(p.reshape(PART // 8, 8, QT), axis=0)

    def values_of(ci, part, acc, p_ref):
        prod = jnp.dot(vt[:, part_slots(ci, part)], p_ref[part_rows(part), :], preferred_element_type=F32)
        return prod if acc is None else acc + prod

    def send_out(n):
        ph, blk, _, flip = tile_place(n)

        @pl.when(stays(n))
        def _():
            land[jnp.where(ph == 1, 2, par(blk)), 0] = obuf[n + 1]

        @pl.when(goes(n))
        def _():
            o_copy(n).start()

        @pl.when(jnp.logical_not(is_worker))
        def _():
            @pl.when(flip == 1)
            def _():
                far_copy(n).start()

            @pl.when(flip == 0)
            def _():
                spot = ph * 2 + par(n)
                far_copy(n).wait_recv()
                both = (obuf[n + 1], passing[spot])
                tops = [p[TOP] for p in both]
                top = jnp.maximum(tops[0], tops[1])
                scales = [jnp.exp2((m - top) * SCALE) for m in tops]
                obuf[n + 1, OUT, :] = scales[0] * both[0][OUT] + scales[1] * both[1][OUT]
                obuf[n + 1, TOP, :] = top
                obuf[n + 1, NORM, :] = scales[0] * both[0][NORM] + scales[1] * both[1][NORM]
                o_copy(n).start()

    sp = ((s0, p0), (s1, p1))
    nparts = CS // PART

    def chunk(state, ci, query):
        m, l, tops, alphas = state
        s_ref, p_ref = sp[ci % 2]
        m_new = tops[0] if ci == 0 else jnp.maximum(m, tops[0])
        alpha_new = jnp.exp2((m - m_new) * SCALE) if ci else jnp.zeros((1, QT), F32)
        l = l * alpha_new
        nxt = acc = None
        for part in range(nparts):
            if alphas is not None:
                acc = values_of((ci - 2) % NCH, part, acc, p_ref)
            l = probs_of(part, m_new, l, s_ref, p_ref)
            if query is not None:
                nxt = scores_of(query, (ci + 2) % NCH, part, nxt, s_ref)
        tops = (tops[1], tops[1] if nxt is None else over_rows(jnp.max, nxt))
        if alphas is None:
            return m_new, l, tops, alpha_new
        oacc[...] = oacc[...] * alphas[0] + acc
        return m_new, l, tops, (alphas[1], alpha_new)

    def put_stats(n, m, l):
        obuf[n + 1, TOP, :] = m
        obuf[n + 1, NORM, :] = over_rows(jnp.sum, l)

    def tile_step(n, carry):
        between(n)
        state = carry[0], carry[1], carry[2:4], carry[4:6]
        q_now, q_next = qbuf[n], qbuf[n + 1]
        for ci in range(2, NCH):
            state = chunk(state, ci, q_now if ci + 2 < NCH else q_next)
        put_stats(n, state[0], state[1])
        for ci in PAIR:
            state = chunk(state, ci, q_next)
        obuf[n + 1, OUT, :] = oacc[...]
        m, l, tops, alphas = state
        return (m, l) + tops + alphas

    def between(n):
        @pl.when(n > 0)
        def _():
            send_out(n - 1)

        @pl.when(n == 0)
        def _():
            send_queries(1, ((1, 1), (1, 0), (0, 1), (0, 0)))
            for dc in range(1, 4):
                kv_copy(dc).start()

        @pl.when(n == ASIDE - 1)
        def _():
            l_wo.wait()
            wait_new()
            for e in PAIR:
                pl.when(is_worker)(functools.partial(new_rows, e, qbuf[par(e, k), :, :HEAD_DIM], (x * 2 + e) * 2 + to))

        @pl.when(jnp.logical_and(n == ASIDE, is_worker))
        def _():
            def first_rows(order, _):
                e = par(k, order)
                wait_parts(e, 1)
                vals = merge(e)
                for i in range(nblk):
                    asend[i, pl.ds(pl.multiple_of(e * ROWS, ROWS), ROWS), :] = jnp.dot(vals, wo[:, block(i, NC)], preferred_element_type=F32)
                    w_copy(e, i).start()
                return 0

            lax.fori_loop(0, 2, first_rows, 0)

        @pl.when(n < 7)
        def _():
            wait_query(n + 1)

    wait_query(0)
    tops = []
    for ci in PAIR:
        top = None
        for part in range(nparts):
            top = scores_of(qbuf[0], ci, part, top, sp[ci][0])
        tops.append(over_rows(jnp.max, top))
    m, l, tops, alpha0 = chunk((None, jnp.zeros((8, QT), F32), tuple(tops), None), 0, qbuf[0])
    m, l, tops, alpha1 = chunk((m, l, tops, None), 1, qbuf[0])
    m, l, top0, top1, alpha0, alpha1 = lax.fori_loop(0, 7, tile_step, (m, l) + tops + (alpha0, alpha1))
    between(7)
    state = m, l, (top0, top1), (alpha0, alpha1)
    for ci in range(2, NCH):
        state = chunk(state, ci, qbuf[7] if ci + 2 < NCH else None)
    put_stats(7, state[0], state[1])
    for ci in PAIR:
        acc = None
        for part in range(nparts):
            acc = values_of(NCH - 2 + ci, part, acc, sp[ci][1])
        oacc[...] = oacc[...] * state[3][ci] + acc
    obuf[8, OUT, :] = oacc[...]
    send_out(7)

    new_rows(2, qown[t], c * 2 + t)
    wait_parts(2, 0)
    vals = merge(2)
    for i in range(nblk):
        hbuf[:, block(i, NC)] = jnp.dot(vals, wo[:, block(i, NC)], preferred_element_type=F32)
    l_g2.wait()
    for i in range(nblk):
        w_copy(0, i).wait_recv()
        cols = block(i, NC)
        hbuf[:, cols] = (x_ref[:, cols].astype(F32) + (hbuf[:, cols] + arecv[i])).astype(BF16).astype(F32)
    mid = hbuf[...]

    place = pl.multiple_of((k * 2 + t) * ROWS, ROWS)
    bbuf[pl.ds(place, ROWS), :] = rms(mid, wide(g2_ref))

    def b_copy(kind, i):
        rows = place if kind < 2 else pl.multiple_of((k * 2 + to) * ROWS, ROWS)
        piece = bbuf.at[pl.ds(rows, ROWS), i * KC:(i + 1) * KC]
        return remote(piece, piece, bs_sem.at[kind, i], br_sem.at[kind, i], partner if kind else ynbr)

    nk = D // KC
    for i in range(nk):
        b_copy(0, i).start()
        b_copy(1, i).start()
    def drain(n, _):
        _, _, _, flip = tile_place(n)
        far = jnp.logical_and(jnp.logical_not(is_worker), flip == 1)

        @pl.when(far)
        def _():
            far_copy(n).wait_send()

        @pl.when(jnp.logical_not(jnp.logical_or(far, stays(n))))
        def _():
            o_copy(n).wait_send()
        return 0

    lax.fori_loop(0, 8, drain, 0)

    @pl.when(is_worker)
    def _():
        for i in range(nblk):
            for e in PAIR:
                w_copy(e, i).wait_send()

    l_wg.wait()
    l_wu.wait()
    nf = FCOLS // 256

    def acc_ref(i):
        if i < 16:
            return (s0, s1)[i // 8].at[i % 8 * 128:(i % 8 + 1) * 128]
        return obuf.at[i - 16, :128]

    cuts = (0, 4, 8, nf)

    def u_copy(i):
        piece = ubuf.at[k, :, cuts[i] * 256:cuts[i + 1] * 256]
        return remote(piece, piece, us_sem.at[i], ur_sem.at[i], partner)

    def forward(i):
        b_copy(0, i).wait_recv()
        b_copy(2, i).start()

    forward(0)
    for i in range(nk):
        if i + 1 < nk:
            forward(i + 1)
        b_copy(1, i).wait_recv()
        b_copy(2, i).wait_recv()
        acts2 = bbuf[:, i * KC:(i + 1) * KC]
        for f in range(nf):
            cols = slice(f * 256, (f + 1) * 256)
            gate = jnp.dot(acts2, wg[i * KC:(i + 1) * KC, cols], preferred_element_type=F32)
            up = jnp.dot(acts2, wu[i * KC:(i + 1) * KC, cols], preferred_element_type=F32)
            if i:
                gate = gate + acc_ref(2 * f)[...]
                up = up + acc_ref(2 * f + 1)[...]
            if i + 1 < nk:
                acc_ref(2 * f)[...] = gate
                acc_ref(2 * f + 1)[...] = up
            else:
                vals = gate / (1.0 + jnp.exp(-gate)) * up
                if f == 0:
                    keep = lax.broadcasted_iota(jnp.int32, (4 * ROWS, 256), 1) >= k * (2 * FCOLS - 5504)
                    vals = jnp.where(keep, vals, 0.0)
                ubuf[k, :, cols] = vals.astype(BF16)
                if f + 1 in cuts:
                    u_copy(cuts.index(f + 1) - 1).start()
    l_wd.wait()

    def d_copy(n):
        piece = asend.at[n * 2 + ko, pl.ds(myrow, ROWS)]
        return remote(piece, drecv.at[n], ds_sem.at[n], dr_sem.at[n], partner)

    def y_copy(n, e):
        piece = asend.at[n * 2 + e, pl.ds(other_row, ROWS)]
        return remote(piece, yrecv.at[k, n], ys_sem.at[n, e], yr_sem.at[k, n], {'cp': x * 2 + e, 'tp': to})

    def down_of(core, n):
        rows = pl.ds(pl.multiple_of(core * (5504 - FCOLS), 128), FCOLS)
        return jnp.dot(ubuf[core], wd[rows, block(n, NC)], preferred_element_type=F32)

    other_row = pl.multiple_of(to * ROWS, ROWS)
    halves = range(nblk // 2)
    for n in halves:
        prod = down_of(k, n)
        for e in PAIR:
            asend[n * 2 + e] = prod[block(e, 64)]
    for i in range(3):
        u_copy(i).wait_recv()
    for n in halves:
        prod = down_of(ko, n)
        for e in PAIR:
            asend[n * 2 + e] = asend[n * 2 + e] + prod[block(e, 64)]
        for e in PAIR:
            y_copy(n, e).start()
        d_copy(n).start()

    def out_copy(core, n):
        cols = pl.ds(pl.multiple_of(core * (D // 2) + n * NC, NC), NC)
        return pltpu.make_async_copy(out_ref.at[:, cols], out_hbm.at[:, cols], out_sem.at[core, n])

    def finish(core, n, base):
        remote(yrecv.at[core, n], yrecv.at[core, n], ys_sem.at[n, 0], yr_sem.at[core, n], ynbr).wait_recv()
        cols = pl.ds(pl.multiple_of(core * (D // 2) + n * NC, NC), NC)
        out_ref[:, cols] = (hbuf[:, cols] + (base + yrecv[core, n])).astype(BF16)
        out_copy(core, n).start()

    for n in halves:
        finish(k, n, asend[n * 2 + k, pl.ds(myrow, ROWS), :])
        d_copy(n).wait_recv()
        finish(ko, n, drecv[n])

    for n in halves:
        for core in (k, ko):
            out_copy(core, n).wait()

    r_v.wait_send()
    r_k.wait_send()
    for ph in PAIR:
        for dx, dy in ((0, 1), (0, 0), (1, 0), (1, 1)):
            if dx or dy:
                q_copy(dx, dy, ph).wait_send()
            else:
                @pl.when(jnp.logical_not(is_worker))
                def _():
                    q_copy(0, 0, ph).wait_send()
    for dc in range(1, 4):
        kv_copy(dc).wait_send()

    for kind in range(3):
        for i in range(nk):
            b_copy(kind, i).wait_send()
    for i in range(3):
        u_copy(i).wait_send()
    for n in halves:
        d_copy(n).wait_send()
        for e in PAIR:
            y_copy(n, e).wait_send()


def solution(mesh):
    token_spec = P(('dp', 'cp', 'tp'), None)
    column_spec = P(None, 'tp')
    row_spec = P('tp', None)

    def device_layer(hidden_loc, pos_loc, cache_len, cache_k, cache_v, norm1_gain, w_query, w_key, w_value, w_out, norm2_gain, w_gate, w_up, w_down):
        inv_freq = 1.0 / (ROPE_BASE ** (jnp.arange(HEAD_DIM // 2, dtype=F32) * (2.0 / HEAD_DIM)))
        freq = jnp.broadcast_to(inv_freq[None, :], (8, HEAD_DIM // 2))
        hbm = pl.BlockSpec(memory_space=pl.ANY)
        dma = pltpu.SemaphoreType.DMA
        return pl.pallas_call(
            kernel,
            out_shape=jax.ShapeDtypeStruct((ROWS, D), BF16),
            in_specs=[pl.BlockSpec(memory_space=pltpu.SMEM)] + [hbm] * 13,
            out_specs=hbm,
            scratch_shapes=[
                pltpu.VMEM((ROWS, D), BF16), pltpu.VMEM((8, 64), F32), pltpu.VMEM((16, 128), BF16), pltpu.VMEM((16, 128), BF16),
                pltpu.VMEM((D, 1024), BF16), pltpu.VMEM((D, 128), BF16), pltpu.VMEM((D, 128), BF16), pltpu.VMEM((1024, D), BF16),
                pltpu.VMEM((D, FCOLS), BF16), pltpu.VMEM((D, FCOLS), BF16), pltpu.VMEM((5504, D // 2), BF16),
                pltpu.VMEM((SLOTS, HEAD_DIM), BF16), pltpu.VMEM((SLOTS, HEAD_DIM), BF16), pltpu.VMEM((HEAD_DIM, SLOTS), BF16),
                pltpu.VMEM((2 * ROWS, D), BF16), pltpu.VMEM((2, QT, HEAD_DIM), BF16), pltpu.VMEM((8, QT, 2 * HEAD_DIM), BF16),
                pltpu.VMEM((4, 2, 64, HEAD_DIM), BF16),
                pltpu.VMEM((CS, QT), F32), pltpu.VMEM((CS, QT), F32), pltpu.VMEM((CS, QT), BF16), pltpu.VMEM((CS, QT), BF16),
                pltpu.VMEM((HEAD_DIM, QT), F32),
                pltpu.VMEM((9, OROWS, QT), F32), pltpu.VMEM((4, OROWS, QT), F32), pltpu.VMEM((3, 3, OROWS, QT), F32), pltpu.VMEM((3, OROWS, QT), F32),
                pltpu.VMEM((ROWS, D), F32), pltpu.VMEM((D // NC, 2 * ROWS, NC), F32), pltpu.VMEM((D // NC, ROWS, NC), F32),
                pltpu.VMEM((4 * ROWS, D), BF16), pltpu.VMEM((2, 4 * ROWS, FCOLS), BF16),
                pltpu.VMEM((2, ROWS, NC), F32), pltpu.VMEM((2, 2, ROWS, NC), F32), pltpu.VMEM((ROWS, D), BF16),
                *(dma(shape) for shape in ((13,), (2,), (2,), (2,), (8,), (8,), (4,), (4,), (8,), (4,), (3, 3), (2, 4), (4,), (3, D // KC), (3, D // KC),
                                           (3,), (3,), (2,), (2,), (2, 2), (2, 2), (2, 2))),
            ],
            compiler_params=pltpu.CompilerParams(collective_id=0, has_side_effects=True, vmem_limit_bytes=67043328),
            name='layer',
        )(cache_len, hidden_loc, freq, norm1_gain.reshape(16, 128), norm2_gain.reshape(16, 128), cache_k, cache_v,
          w_query, w_key, w_value, w_out, w_gate, w_up, w_down)

    return jax.shard_map(device_layer, mesh=mesh, in_specs=(token_spec, P(('dp', 'cp', 'tp')), P('dp'), token_spec, token_spec, P(), column_spec, column_spec, column_spec, row_spec, P(), column_spec, column_spec, row_spec), out_specs=token_spec, check_vma=False)
```

time: 321 us -> 59.1 us (0.18)
  matrix products: 101 us -> 0 us
  blocking collectives: 94.4 us -> 0 us
  waiting for transfers between devices: 69.3 us -> 0 us
  Pallas kernels: 0 us -> 56.1 us
  other arithmetic: 33.8 us -> 0.01 us
  between operations: 14.5 us -> 0.67 us
  local copies, waits for them, and re-layouts: 6.94 us -> 2.17 us
    dot_general x14 -> x0, matrix products: 101 us -> none  [the longest x2 33 us: attend_rows(): jnp.einsum('rkgd,skd->krgs', block_queries, cache_keys, preferred_element...]
    all_to_all x2 -> x0, blocking collectives: 58.2 us -> none  [the longest x1 30.2 us: device_layer(): lax.all_to_all(cache_v, 'tp', 1, 0, tiled=True)]
    pallas_call x0 -> x1, Pallas kernels: none -> 56.1 us  [device_layer(): pl.pallas_call(kernel, out_shape=jax.ShapeDtypeStruct((ROWS, D), BF16), i...]
    all_gather x2 -> x0, waiting for transfers between devices: 45.6 us -> none  [the longest x1 45.6 us: device_layer(): lax.all_gather(lax.all_to_all(cache_k, 'tp', 1, 0, tiled=True), 'cp', axi...]
    reduce_sum x6 -> x0, other arithmetic: 29.7 us -> none  [the longest x2 28.1 us: attend_rows(): jnp.sum(cache_probs, axis=-1, keepdims=True)]
    all_gather x4 -> x0, blocking collectives: 27.1 us -> none  [the longest x1 8.1 us: device_layer(): new_values = lax.all_gather(values_loc, 'cp', axis=0, tiled=True)]
    reduce_scatter x2 -> x0, waiting for transfers between devices: 23.6 us -> none  [the longest x1 11.9 us: device_layer(): lax.psum_scatter(mlp_part, 'tp', scatter_dimension=0, tiled=True)]
    unnamed x2 -> x0, blocking collectives: 9.13 us -> none
  transfers between devices with their start and end apart: 4 -> 0, of which waited for: 3 -> 0; matrix products, arithmetic and copies ran while one was open for 3% -> 0% of each run, Pallas kernels for 0% -> 0%
where the time goes in v2:
time: 59.1 us; the launch traced here: 58.9 us
  Pallas kernels  56.1 us (95%)
  local copies, waits for them, and re-layouts  2.17 us (4%)
  between operations  0.67 us (1%)
    pallas_call x1, Pallas kernels, device_layer(): pl.pallas_call(kernel, out_shape=jax.ShapeDtypeStruct((ROWS, D), BF16), i...  56.1 us
    unnamed x1, local copies, waits for them, and re-layouts  1.57 us

profile of v2, /device:TPU:0, one launch (start us, length us, event | category | flops | bytes accessed | tf_op | source)
XLA Modules:
  0.0 58.9 jit_solution(2984791061543818686)
XLA Ops:
  0.7 0.6 %broadcast_in_dim.2.freq_hbm = f32[8,64]{1,0:T(8,128)} broadcast(f32[64]{0:T(128)S(1)} %negate_power_fusion), dimensions={1} | broadcast | bytes 2304 | tf_op jit(solution)/shard_map/broadcast_in_dim | solution.py:619
  1.3 56.1 %layer.1 = bf16[32,2048]{1,0:T(8,128)(2,1)} custom-call(s32[1]{0:T(128)S(6)} %copy.15.len_ref, bf16[32,2048]{1,0:T(8,128)(2,1)} %x_hbm.1, f32[8,64]{1,0:T(8,128)} %broadcast_in_dim.2.freq_hbm, bf16[16,128]{1,0:T(8,128)(2,1)} %bitcast.2, bf16[16,128]{1,0:T(8,128)(2,1)} %bitcast.3, bf16[4096,256]{1,0:T(8,128)(2,1)} %ck_ref.1, bf16[4096,256]{1,0:T(8,128)(2,1)} %cv_ref.1, ...), custom_call_target="tpu_custom_call" | custom-call | tf_op jit(solution)/shard_map/layer/pallas_call | solution.py:622
  57.4 1.6 %copy.16 = bf16[32,2048]{1,0:T(8,128)(2,1)} copy(bf16[32,2048]{1,0:T(8,128)(2,1)} %layer.1) | data formatting | bytes 262144
  (1 shorter events, 0.0 us)

commit v3 on v2

--- a/solution.py
+++ b/solution.py
@@ -1,4 +1,5 @@
 import functools
+import itertools
 import math
 import operator
 
@@ -25,7 +26,7 @@
 CS = 1024
 NCH = SLOTS // CS
 VT = 512
-ASIDE = 6
+ASIDE = 5
 KC = 512
 NC = 512
 PART = 512
@@ -86,7 +87,7 @@
            out_hbm,
            x_ref, freq_ref, g1_ref, g2_ref, wq, wk, wv, wo, wg, wu, wd, kbuf, vbuf, vt, abuf, qown, qbuf, kvbuf, s0, s1, p0, p1, oacc, obuf, passing, land, newo, hbuf, asend, arecv,
            bbuf, ubuf, drecv, yrecv, out_ref,
-           ld_sem, cs_sem, cr_sem, a_sem, qs_sem, qr_sem, kvs_sem, kvr_sem, os_sem, ps_sem, or_sem, ws_sem, wr_sem, bs_sem, br_sem,
+           ld_sem, cs_sem, cr_sem, as_sem, ar_sem, qs_sem, qr_sem, kvs_sem, kvr_sem, os_sem, ps_sem, or_sem, ws_sem, wr_sem, bs_sem, br_sem,
            us_sem, ur_sem, ds_sem, dr_sem, ys_sem, yr_sem, out_sem):
     c = lax.axis_index('cp')
     t = lax.axis_index('tp')
@@ -135,8 +136,12 @@
     abuf[pl.ds(myrow, ROWS), :] = rms(x_ref[...].astype(F32), g1)
 
     pl.semaphore_wait(barrier, 7)
-    a_copy = remote(abuf.at[pl.ds(myrow, ROWS), :], abuf.at[pl.ds(myrow, ROWS), :], a_sem.at[0], a_sem.at[1], ynbr)
-    a_copy.start()
+    def a_copy(i):
+        piece = abuf.at[pl.ds(myrow, ROWS), block(i, D // 2)]
+        return remote(piece, piece, as_sem.at[i], ar_sem.at[i], ynbr)
+
+    for i in PAIR:
+        a_copy(i).start()
     r_v = remote(cv_ref.at[:, pl.ds(kocol, HEAD_DIM)], vbuf.at[pl.ds(myhalf, HALF), :], cs_sem.at[0], cr_sem.at[0], partner)
     r_k = remote(ck_ref.at[:, pl.ds(kocol, HEAD_DIM)], kbuf.at[pl.ds(myhalf, HALF), :], cs_sem.at[1], cr_sem.at[1], partner)
     r_v.start()
@@ -173,45 +178,51 @@
     l_wv.wait()
     for copy in (l_wo, l_wg, l_wu, l_wd):
         copy.start()
-    a_copy.wait()
-    acts = abuf[...]
     cos = jnp.concatenate([cos, cos], axis=1)
     sin = jnp.concatenate([-sin, sin], axis=1)
 
     def rope(vals):
         return (vals * cos + pltpu.roll(vals, HEAD_DIM // 2, 1) * sin).astype(BF16)
 
-    for hp in range(HEADS // 2):
-        prod = jnp.dot(acts, wq[:, hp * 256:(hp + 1) * 256], preferred_element_type=F32)
-        for sub in PAIR:
-            h = hp * 2 + sub
-            rot = rope(prod[:, sub * HEAD_DIM:(sub + 1) * HEAD_DIM])
-            qown[0, h * ROWS:(h + 1) * ROWS, :] = rot[:ROWS]
-            qown[1, h * ROWS:(h + 1) * ROWS, :] = rot[ROWS:]
-
-    def q_copy(dx, dy, ph):
+    def q_copy(dx, dy, ph, half):
         j = to if ph == 0 else t
         dev = {'cp': par(x, dx) * 2 + t, 'tp': par(t, dy)}
         n = (dx * 2 + dy) * 2 + ph
         tile = ph * 4 + (dx + max(dy, ph)) % 2 * 2 + par(k, t, ph)
-        return remote(qown.at[j], qbuf.at[tile, :, :HEAD_DIM], qs_sem.at[n], qr_sem.at[tile], dev)
-
-    def send_queries(ph, places):
+        rows = block(half, QT // 2)
+        return remote(qown.at[j, rows], qbuf.at[tile, rows, :HEAD_DIM], qs_sem.at[n, half], qr_sem.at[tile, half], dev)
+
+    def send_queries(ph, places, half):
         for dx, dy in places:
+            copy = q_copy(dx, dy, ph, half)
             if dx or dy:
-                q_copy(dx, dy, ph).start()
+                copy.start()
             else:
-                @pl.when(jnp.logical_not(is_worker))
-                def _():
-                    q_copy(0, 0, ph).start()
-
-    send_queries(0, ((1, 1), (0, 0)))
+                pl.when(jnp.logical_not(is_worker))(copy.start)
+
+    for i in PAIR:
+        a_copy(i).wait()
+        acts = abuf[:, block(i, D // 2)]
+        for hp in range(HEADS // 2):
+            prod = jnp.dot(acts, wq[block(i, D // 2), block(hp, 256)], preferred_element_type=F32)
+            if i == 0:
+                s0[block(hp, 64), :] = prod
+                continue
+            prod = prod + s0[block(hp, 64), :]
+            for sub in PAIR:
+                rot = rope(prod[:, block(sub, HEAD_DIM)])
+                for j in PAIR:
+                    qown[j, block(hp * 2 + sub, ROWS), :] = rot[block(j, ROWS)]
+            if hp % 2:
+                send_queries(0, ((1, 1), (0, 0)), hp // 2)
+
 
     @pl.when(is_worker)
     def _():
         qbuf[0, :, :HEAD_DIM] = qown[to]
         qbuf[7, :, :HEAD_DIM] = qown[t]
 
+    acts = abuf[...]
     kvbuf[c, 0] = rope(jnp.dot(acts, wk[...], preferred_element_type=F32))
     kvbuf[c, 1] = jnp.dot(acts, wv[...], preferred_element_type=F32).astype(BF16)
 
@@ -220,7 +231,12 @@
 
     r_v.wait_recv()
     turn_half(ko)
-    send_queries(0, ((0, 1), (1, 0)))
+    for half in PAIR:
+        send_queries(0, ((0, 1), (1, 0)), half)
+    for dc in range(1, 4):
+        kv_copy(dc).start()
+    for half in PAIR:
+        send_queries(1, ((1, 1), (1, 0), (0, 1), (0, 0)), half)
     l_k.wait()
     r_k.wait_recv()
 
@@ -295,7 +311,9 @@
     def wait_query(n):
         @pl.when(jnp.logical_not(jnp.logical_and(is_worker, lax.rem(n, 7) == 0)))
         def _():
-            remote(qown.at[0], qbuf.at[n, :, :HEAD_DIM], qs_sem.at[0], qr_sem.at[n], ynbr).wait_recv()
+            for half in PAIR:
+                rows = block(half, QT // 2)
+                remote(qown.at[0, rows], qbuf.at[n, rows, :HEAD_DIM], qs_sem.at[0, half], qr_sem.at[n, half], ynbr).wait_recv()
 
     def part_rows(part):
         return slice(part * PART, (part + 1) * PART)
@@ -394,12 +412,6 @@
         def _():
             send_out(n - 1)
 
-        @pl.when(n == 0)
-        def _():
-            send_queries(1, ((1, 1), (1, 0), (0, 1), (0, 0)))
-            for dc in range(1, 4):
-                kv_copy(dc).start()
-
         @pl.when(n == ASIDE - 1)
         def _():
             l_wo.wait()
@@ -407,18 +419,14 @@
             for e in PAIR:
                 pl.when(is_worker)(functools.partial(new_rows, e, qbuf[par(e, k), :, :HEAD_DIM], (x * 2 + e) * 2 + to))
 
-        @pl.when(jnp.logical_and(n == ASIDE, is_worker))
-        def _():
-            def first_rows(order, _):
-                e = par(k, order)
-                wait_parts(e, 1)
-                vals = merge(e)
-                for i in range(nblk):
-                    asend[i, pl.ds(pl.multiple_of(e * ROWS, ROWS), ROWS), :] = jnp.dot(vals, wo[:, block(i, NC)], preferred_element_type=F32)
-                    w_copy(e, i).start()
-                return 0
-
-            lax.fori_loop(0, 2, first_rows, 0)
+        @pl.when(is_worker & (n >= ASIDE) & (n < ASIDE + 2))
+        def _():
+            e = par(k, n - ASIDE)
+            wait_parts(e, 1)
+            vals = merge(e)
+            for i in range(nblk):
+                asend[i, pl.ds(pl.multiple_of(e * ROWS, ROWS), ROWS), :] = jnp.dot(vals, wo[:, block(i, NC)], preferred_element_type=F32)
+                w_copy(e, i).start()
 
         @pl.when(n < 7)
         def _():
@@ -462,14 +470,20 @@
     place = pl.multiple_of((k * 2 + t) * ROWS, ROWS)
     bbuf[pl.ds(place, ROWS), :] = rms(mid, wide(g2_ref))
 
+    def b_piece(rows, i):
+        return bbuf.at[pl.ds(rows, ROWS), block(i, KC)]
+
     def b_copy(kind, i):
         rows = place if kind < 2 else pl.multiple_of((k * 2 + to) * ROWS, ROWS)
-        piece = bbuf.at[pl.ds(rows, ROWS), i * KC:(i + 1) * KC]
+        piece = b_piece(rows, i)
         return remote(piece, piece, bs_sem.at[kind, i], br_sem.at[kind, i], partner if kind else ynbr)
 
     nk = D // KC
+    b_direct = remote(b_piece(place, 0), b_piece(place, 0), bs_sem.at[2, 0], br_sem.at[2, 0], {'cp': x * 2 + ko, 'tp': to})
     for i in range(nk):
         b_copy(0, i).start()
+        if i == 0:
+            b_direct.start()
         b_copy(1, i).start()
     def drain(n, _):
         _, _, _, flip = tile_place(n)
@@ -509,7 +523,8 @@
 
     def forward(i):
         b_copy(0, i).wait_recv()
-        b_copy(2, i).start()
+        if i:
+            b_copy(2, i).start()
 
     forward(0)
     for i in range(nk):
@@ -529,7 +544,7 @@
                 acc_ref(2 * f)[...] = gate
                 acc_ref(2 * f + 1)[...] = up
             else:
-                vals = gate / (1.0 + jnp.exp(-gate)) * up
+                vals = gate / (1.0 + jnp.exp2(gate * -math.log2(math.e))) * up
                 if f == 0:
                     keep = lax.broadcasted_iota(jnp.int32, (4 * ROWS, 256), 1) >= k * (2 * FCOLS - 5504)
                     vals = jnp.where(keep, vals, 0.0)
@@ -587,14 +602,13 @@
 
     r_v.wait_send()
     r_k.wait_send()
-    for ph in PAIR:
-        for dx, dy in ((0, 1), (0, 0), (1, 0), (1, 1)):
+    for half in PAIR:
+        for ph, dx, dy in itertools.product(PAIR, PAIR, PAIR):
+            copy = q_copy(dx, dy, ph, half)
             if dx or dy:
-                q_copy(dx, dy, ph).wait_send()
+                copy.wait_send()
             else:
-                @pl.when(jnp.logical_not(is_worker))
-                def _():
-                    q_copy(0, 0, ph).wait_send()
+                pl.when(jnp.logical_not(is_worker))(copy.wait_send)
     for dc in range(1, 4):
         kv_copy(dc).wait_send()
 
@@ -637,7 +651,7 @@
                 pltpu.VMEM((ROWS, D), F32), pltpu.VMEM((D // NC, 2 * ROWS, NC), F32), pltpu.VMEM((D // NC, ROWS, NC), F32),
                 pltpu.VMEM((4 * ROWS, D), BF16), pltpu.VMEM((2, 4 * ROWS, FCOLS), BF16),
                 pltpu.VMEM((2, ROWS, NC), F32), pltpu.VMEM((2, 2, ROWS, NC), F32), pltpu.VMEM((ROWS, D), BF16),
-                *(dma(shape) for shape in ((13,), (2,), (2,), (2,), (8,), (8,), (4,), (4,), (8,), (4,), (3, 3), (2, 4), (4,), (3, D // KC), (3, D // KC),
+                *(dma(shape) for shape in ((13,), (2,), (2,), (2,), (2,), (8, 2), (8, 2), (4,), (4,), (8,), (4,), (3, 3), (2, 4), (4,), (3, D // KC), (3, D // KC),
                                            (3,), (3,), (2,), (2,), (2, 2), (2, 2), (2, 2))),
             ],
             compiler_params=pltpu.CompilerParams(collective_id=0, has_side_effects=True, vmem_limit_bytes=67043328),

time: 59.1 us -> 58.5 us (0.990)
  no operation moved by 1% of the time
where the time goes in v3:
time: 58.5 us; the launch traced here: 58.4 us
  Pallas kernels  55.6 us (95%)
  local copies, waits for them, and re-layouts  2.17 us (4%)
  between operations  0.67 us (1%)
    pallas_call x1, Pallas kernels, device_layer(): pl.pallas_call(kernel, out_shape=jax.ShapeDtypeStruct((ROWS, D), BF16), i...  55.6 us
    unnamed x1, local copies, waits for them, and re-layouts  1.57 us

profile of v3, /device:TPU:0, one launch (start us, length us, event | category | flops | bytes accessed | tf_op | source)
XLA Modules:
  0.0 58.4 jit_solution(11802395460549213644)
XLA Ops:
  0.7 0.6 %broadcast_in_dim.2.freq_hbm = f32[8,64]{1,0:T(8,128)} broadcast(f32[64]{0:T(128)S(1)} %negate_power_fusion), dimensions={1} | broadcast | bytes 2304 | tf_op jit(solution)/shard_map/broadcast_in_dim | solution.py:633
  1.3 55.6 %layer.1 = bf16[32,2048]{1,0:T(8,128)(2,1)} custom-call(s32[1]{0:T(128)S(6)} %copy.15.len_ref, bf16[32,2048]{1,0:T(8,128)(2,1)} %x_hbm.1, f32[8,64]{1,0:T(8,128)} %broadcast_in_dim.2.freq_hbm, bf16[16,128]{1,0:T(8,128)(2,1)} %bitcast.2, bf16[16,128]{1,0:T(8,128)(2,1)} %bitcast.3, bf16[4096,256]{1,0:T(8,128)(2,1)} %ck_ref.1, bf16[4096,256]{1,0:T(8,128)(2,1)} %cv_ref.1, ...), custom_call_target="tpu_custom_call" | custom-call | tf_op jit(solution)/shard_map/layer/pallas_call | solution.py:636
  56.8 1.6 %copy.16 = bf16[32,2048]{1,0:T(8,128)(2,1)} copy(bf16[32,2048]{1,0:T(8,128)(2,1)} %layer.1) | data formatting | bytes 262144
  (1 shorter events, 0.0 us)

commit v4 on v3

--- a/solution.py
+++ b/solution.py
@@ -37,6 +37,9 @@
 PAIR = range(2)
 OUT, TOP, NORM = (slice(*b) for b in ((0, HEAD_DIM), (HEAD_DIM, HEAD_DIM + 1), (HEAD_DIM + 1, HEAD_DIM + 2)))
 CONTRACT_LAST = (((1,), (1,)), ((), ()))
+FREQ = 2 * math.log2(ROPE_BASE) / HEAD_DIM
+FREQ_A = round(FREQ * 2 ** 16) / 2 ** 16
+FREQ_B = FREQ - FREQ_A
 PI_A = 201.0 / 128.0
 PI_B = round((math.pi / 2 - PI_A) * 2.0 ** 20) / 2.0 ** 20
 PI_C = math.pi / 2 - PI_A - PI_B
@@ -47,6 +50,17 @@
     dev, high = index >> 5, (index >> 4) & 1
     seg = dev + high * (15 - 2 * dev)
     return seg * half + (index & (half - 1))
+
+
+def frequencies():
+    lane = lax.broadcasted_iota(jnp.int32, (8, HEAD_DIM // 2), 1).astype(F32)
+    whole = lane * FREQ_A
+    n = jnp.floor(whole + 0.5)
+    power = ((n - whole) - lane * FREQ_B) * math.log(2)
+    series = 1.0
+    for d in range(8, 0, -1):
+        series = 1.0 + power * (1 / d) * series
+    return series * jnp.exp2(-n)
 
 
 def turn(angle):
@@ -83,9 +97,9 @@
     return (values * inv * gain).astype(BF16)
 
 
-def kernel(len_ref, x_hbm, freq_hbm, g1_hbm, g2_hbm, ck_ref, cv_ref, wq_hbm, wk_hbm, wv_hbm, wo_hbm, wg_hbm, wu_hbm, wd_hbm,
+def kernel(len_ref, x_hbm, g1_hbm, g2_hbm, ck_ref, cv_ref, wq_hbm, wk_hbm, wv_hbm, wo_hbm, wg_hbm, wu_hbm, wd_hbm,
            out_hbm,
-           x_ref, freq_ref, g1_ref, g2_ref, wq, wk, wv, wo, wg, wu, wd, kbuf, vbuf, vt, abuf, qown, qbuf, kvbuf, s0, s1, p0, p1, oacc, obuf, passing, land, newo, hbuf, asend, arecv,
+           x_ref, g1_ref, g2_ref, wq, wk, wv, wo, wg, wu, wd, kbuf, vbuf, vt, abuf, qown, qbuf, kvbuf, s0, s1, p0, p1, oacc, obuf, passing, land, newo, hbuf, asend, arecv,
            bbuf, ubuf, drecv, yrecv, out_ref,
            ld_sem, cs_sem, cr_sem, as_sem, ar_sem, qs_sem, qr_sem, kvs_sem, kvr_sem, os_sem, ps_sem, or_sem, ws_sem, wr_sem, bs_sem, br_sem,
            us_sem, ur_sem, ds_sem, dr_sem, ys_sem, yr_sem, out_sem):
@@ -125,8 +139,7 @@
     l_x = local(x_hbm, x_ref, 9)
     l_g1 = local(g1_hbm, g1_ref, 10)
     l_g2 = local(g2_hbm, g2_ref, 11)
-    l_freq = local(freq_hbm, freq_ref, 12)
-    for copy in (l_x, l_g1, l_wq, l_v, l_wk, l_wv, l_freq, l_k, l_g2):
+    for copy in (l_x, l_g1, l_wq, l_v, l_wk, l_wv, l_k, l_g2):
         copy.start()
 
     l_x.wait()
@@ -168,9 +181,8 @@
     one_col = (lax.broadcasted_iota(jnp.int32, (QT, HEAD_DIM), 1) == 0).astype(F32).astype(BF16)
     for n in range(8):
         qbuf[n, :, HEAD_DIM:] = one_col
-    l_freq.wait()
     pos = clen + rel_position(c * 64 + lax.broadcasted_iota(jnp.int32, (64, HEAD_DIM // 2), 0))
-    cos, sin = turn(pos.astype(F32) * freq_ref[0:1, :])
+    cos, sin = turn(pos.astype(F32) * frequencies()[:1])
     oacc[...] = jnp.zeros((HEAD_DIM, QT), F32)
 
     l_wq.wait()
@@ -629,17 +641,15 @@
     row_spec = P('tp', None)
 
     def device_layer(hidden_loc, pos_loc, cache_len, cache_k, cache_v, norm1_gain, w_query, w_key, w_value, w_out, norm2_gain, w_gate, w_up, w_down):
-        inv_freq = 1.0 / (ROPE_BASE ** (jnp.arange(HEAD_DIM // 2, dtype=F32) * (2.0 / HEAD_DIM)))
-        freq = jnp.broadcast_to(inv_freq[None, :], (8, HEAD_DIM // 2))
         hbm = pl.BlockSpec(memory_space=pl.ANY)
         dma = pltpu.SemaphoreType.DMA
         return pl.pallas_call(
             kernel,
             out_shape=jax.ShapeDtypeStruct((ROWS, D), BF16),
-            in_specs=[pl.BlockSpec(memory_space=pltpu.SMEM)] + [hbm] * 13,
+            in_specs=[pl.BlockSpec(memory_space=pltpu.SMEM)] + [hbm] * 12,
             out_specs=hbm,
             scratch_shapes=[
-                pltpu.VMEM((ROWS, D), BF16), pltpu.VMEM((8, 64), F32), pltpu.VMEM((16, 128), BF16), pltpu.VMEM((16, 128), BF16),
+                pltpu.VMEM((ROWS, D), BF16), pltpu.VMEM((16, 128), BF16), pltpu.VMEM((16, 128), BF16),
                 pltpu.VMEM((D, 1024), BF16), pltpu.VMEM((D, 128), BF16), pltpu.VMEM((D, 128), BF16), pltpu.VMEM((1024, D), BF16),
                 pltpu.VMEM((D, FCOLS), BF16), pltpu.VMEM((D, FCOLS), BF16), pltpu.VMEM((5504, D // 2), BF16),
                 pltpu.VMEM((SLOTS, HEAD_DIM), BF16), pltpu.VMEM((SLOTS, HEAD_DIM), BF16), pltpu.VMEM((HEAD_DIM, SLOTS), BF16),
@@ -656,7 +666,7 @@
             ],
             compiler_params=pltpu.CompilerParams(collective_id=0, has_side_effects=True, vmem_limit_bytes=67043328),
             name='layer',
-        )(cache_len, hidden_loc, freq, norm1_gain.reshape(16, 128), norm2_gain.reshape(16, 128), cache_k, cache_v,
+        )(cache_len, hidden_loc, norm1_gain.reshape(16, 128), norm2_gain.reshape(16, 128), cache_k, cache_v,
           w_query, w_key, w_value, w_out, w_gate, w_up, w_down)
 
     return jax.shard_map(device_layer, mesh=mesh, in_specs=(token_spec, P(('dp', 'cp', 'tp')), P('dp'), token_spec, token_spec, P(), column_spec, column_spec, column_spec, row_spec, P(), column_spec, column_spec, row_spec), out_specs=token_spec, check_vma=False)

time: 58.5 us -> 58.1 us (level)
  local copies, waits for them, and re-layouts: 2.17 us -> 1.57 us
    broadcast_in_dim x1 -> x0, local copies, waits for them, and re-layouts: 0.6 us -> none  [device_layer(): freq = jnp.broadcast_to(inv_freq[None, :], (8, HEAD_DIM // 2))]
where the time goes in v4:
time: 58.1 us; the launch traced here: 58 us
  Pallas kernels  55.8 us (96%)
  local copies, waits for them, and re-layouts  1.57 us (3%)
  between operations  0.66 us (1%)
    pallas_call x1, Pallas kernels, device_layer(): pl.pallas_call(kernel, out_shape=jax.ShapeDtypeStruct((ROWS, D), BF16), i...  55.8 us
    unnamed x1, local copies, waits for them, and re-layouts  1.57 us

profile of v4, /device:TPU:0, one launch (start us, length us, event | category | flops | bytes accessed | tf_op | source)
XLA Modules:
  0.0 58.0 jit_solution(10790644933597585736)
XLA Ops:
  0.7 55.8 %layer.1 = bf16[32,2048]{1,0:T(8,128)(2,1)} custom-call(s32[1]{0:T(128)S(6)} %copy.15.len_ref, bf16[32,2048]{1,0:T(8,128)(2,1)} %x_hbm.1, bf16[16,128]{1,0:T(8,128)(2,1)} %bitcast.2, bf16[16,128]{1,0:T(8,128)(2,1)} %bitcast.3, bf16[4096,256]{1,0:T(8,128)(2,1)} %ck_ref.1, bf16[4096,256]{1,0:T(8,128)(2,1)} %cv_ref.1, bf16[2048,1024]{1,0:T(8,128)(2,1)} %wq_hbm.1, ...), custom_call_target="tpu_custom_call" | custom-call | tf_op jit(solution)/shard_map/layer/pallas_call | solution.py:646
  56.4 1.6 %copy.16 = bf16[32,2048]{1,0:T(8,128)(2,1)} copy(bf16[32,2048]{1,0:T(8,128)(2,1)} %layer.1) | data formatting | bytes 262144

commit v5 on v4

--- a/solution.py
+++ b/solution.py
@@ -139,7 +139,7 @@
     l_x = local(x_hbm, x_ref, 9)
     l_g1 = local(g1_hbm, g1_ref, 10)
     l_g2 = local(g2_hbm, g2_ref, 11)
-    for copy in (l_x, l_g1, l_wq, l_v, l_wk, l_wv, l_k, l_g2):
+    for copy in (l_x, l_g1, l_v, l_k, l_wq, l_wk, l_wv, l_g2):
         copy.start()
 
     l_x.wait()
@@ -168,14 +168,17 @@
     def turn_half(core):
         def body(i, _):
             off = pl.multiple_of(core * HALF + i * VT, VT)
-            vals = vbuf[pl.ds(off, VT), :]
+            rows = pl.ds(off, VT)
+            gone = rowi + (HALF * (4 * x + 2 * core + t) + i * VT) >= clen
+            vals = jnp.where(gone, 0.0, vbuf[rows, :].astype(F32)).astype(BF16)
+            kbuf[rows, :] = jnp.where(gone, 0.0, kbuf[rows, :].astype(F32)).astype(BF16)
             vt[:, pl.ds(off, VT)] = lax.dot_general(eye, vals, CONTRACT_LAST, preferred_element_type=F32).astype(BF16)
-            hidden = (rowi + (HALF * (4 * x + 2 * core + t) + i * VT) >= clen) & lane0
-            vbuf[pl.ds(off, VT), :] = jnp.where(hidden, NEG, 0.0).astype(BF16)
+            vbuf[rows, :] = jnp.where(gone & lane0, NEG, 0.0).astype(BF16)
             return 0
         lax.fori_loop(0, HALF // VT, body, 0)
 
     l_v.wait()
+    l_k.wait()
     turn_half(k)
 
     one_col = (lax.broadcasted_iota(jnp.int32, (QT, HEAD_DIM), 1) == 0).astype(F32).astype(BF16)
@@ -242,6 +245,7 @@
         return remote(kvbuf.at[c], kvbuf.at[c], kvs_sem.at[dc], kvr_sem.at[c], {'cp': lax.rem(c + dc, 4), 'tp': t})
 
     r_v.wait_recv()
+    r_k.wait_recv()
     turn_half(ko)
     for half in PAIR:
         send_queries(0, ((0, 1), (1, 0)), half)
@@ -249,8 +253,6 @@
         kv_copy(dc).start()
     for half in PAIR:
         send_queries(1, ((1, 1), (1, 0), (0, 1), (0, 0)), half)
-    l_k.wait()
-    r_k.wait_recv()
 
     nblk = D // NC
 
@@ -527,7 +529,7 @@
             return (s0, s1)[i // 8].at[i % 8 * 128:(i % 8 + 1) * 128]
         return obuf.at[i - 16, :128]
 
-    cuts = (0, 4, 8, nf)
+    cuts = (0, 5, 9, nf)
 
     def u_copy(i):
         piece = ubuf.at[k, :, cuts[i] * 256:cuts[i + 1] * 256]

time: 58.1 us -> 58.3 us (level)
  no operation moved by 1% of the time
where the time goes in v5:
time: 58.3 us; the launch traced here: 58.2 us
  Pallas kernels  56 us (96%)
  local copies, waits for them, and re-layouts  1.57 us (3%)
  between operations  0.66 us (1%)
    pallas_call x1, Pallas kernels, device_layer(): pl.pallas_call(kernel, out_shape=jax.ShapeDtypeStruct((ROWS, D), BF16), i...  56 us
    unnamed x1, local copies, waits for them, and re-layouts  1.57 us

profile of v5, /device:TPU:0, one launch (start us, length us, event | category | flops | bytes accessed | tf_op | source)
XLA Modules:
  0.0 58.2 jit_solution(15898259135322731580)
XLA Ops:
  0.7 56.0 %layer.1 = bf16[32,2048]{1,0:T(8,128)(2,1)} custom-call(s32[1]{0:T(128)S(6)} %copy.15.len_ref, bf16[32,2048]{1,0:T(8,128)(2,1)} %x_hbm.1, bf16[16,128]{1,0:T(8,128)(2,1)} %bitcast.2, bf16[16,128]{1,0:T(8,128)(2,1)} %bitcast.3, bf16[4096,256]{1,0:T(8,128)(2,1)} %ck_ref.1, bf16[4096,256]{1,0:T(8,128)(2,1)} %cv_ref.1, bf16[2048,1024]{1,0:T(8,128)(2,1)} %wq_hbm.1, ...), custom_call_target="tpu_custom_call" | custom-call | tf_op jit(solution)/shard_map/layer/pallas_call | solution.py:648
  56.6 1.6 %copy.16 = bf16[32,2048]{1,0:T(8,128)(2,1)} copy(bf16[32,2048]{1,0:T(8,128)(2,1)} %layer.1) | data formatting | bytes 262144
